TPU v7x, 8 devices: a whole 2x2x1 slice. The times are simulated.
8 devices in a mesh: dp: 1 (over z), cp: 8 (over y, x, core).
Axes of the slice: x: 2, y: 2, z: 1, core: 2. Of those that a mesh axis runs over, the one named last changes fastest.
Arguments:
- x_in: bfloat16 [1, 6144, 2048], P('dp', 'cp')
- positions: int32 [6144], P(('dp', 'cp'))
- long_factor: float32 [32], replicated
- norm_gain: float32 [2048], replicated
- w_qkv: bfloat16 [2048, 6144], replicated
- w_out: bfloat16 [2048, 2048], replicated
- grad_y: bfloat16 [1, 6144, 2048], P('dp', 'cp')
Outputs:
- output 1: bfloat16 [1, 6144, 2048], P('dp', 'cp')
- output 2: bfloat16 [1, 6144, 2048], P('dp', 'cp')
- output 3: float32 [2048], P('dp')
- output 4: float32 [2048, 6144], P('dp')
- output 5: float32 [2048, 2048], P('dp')
All inputs are finite; a program needn't handle non-finite values.
Results may differ from a plain program's by a relative error of at most 0.0138761.
Values are sent between devices in bfloat16 or wider.
A program may use at most 1 GiB of HBM per device.

v0:
```python
import math
import jax
import jax.numpy as jnp
from jax import lax
from jax.sharding import PartitionSpec as P

NORM_EPS = 1e-5
MSCALE = math.sqrt(1.0 + math.log(32.0) / math.log(4096.0))
MASK_VALUE = -1e30


def rope_tables(positions, long_factor):
    half = long_factor.shape[0]
    exponent = jnp.arange(half, dtype=jnp.float32) * (1.0 / half)
    inv_freq = 1.0 / (long_factor * jnp.power(10000.0, exponent))
    angles = positions.astype(jnp.float32)[:, None] * inv_freq[None, :]
    angle_pair = jnp.concatenate([angles, angles], axis=-1)
    return (jnp.cos(angle_pair) * MSCALE)[None, :, None, :], (jnp.sin(angle_pair) * MSCALE)[None, :, None, :]


def rotate_half(values):
    half = values.shape[-1] // 2
    return jnp.concatenate([-values[..., half:], values[..., :half]], axis=-1)


def masked_scores(q_blk, k_blk, q_start, k_start, scale):
    scores = jnp.einsum('bqhd,bkhd->bhqk', q_blk, k_blk, preferred_element_type=jnp.float32) * scale
    q_pos = q_start + jnp.arange(q_blk.shape[1])[:, None]
    k_pos = k_start + jnp.arange(k_blk.shape[1])[None, :]
    return jnp.where(k_pos <= q_pos, scores, MASK_VALUE)


def fwd_block(stats, q_blk, k_blk, v_blk, q_start, k_start, scale):
    out_acc, row_max, row_sum = stats
    scores = masked_scores(q_blk, k_blk, q_start, k_start, scale)
    new_max = jnp.maximum(row_max, jnp.max(scores, axis=-1, keepdims=True))
    rescale = jnp.exp(row_max - new_max)
    attn_probs = jnp.exp(scores - new_max)
    row_sum = row_sum * rescale + jnp.sum(attn_probs, axis=-1, keepdims=True)
    pv_part = jnp.einsum('bhqk,bkhd->bqhd', attn_probs.astype(jnp.bfloat16), v_blk, preferred_element_type=jnp.float32)
    out_acc = out_acc * jnp.transpose(rescale, (0, 2, 1, 3)) + pv_part
    return out_acc, new_max, row_sum


def bwd_block(q_blk, k_blk, v_blk, d_attn, log_norm, delta, q_start, k_start, scale):
    attn_probs = jnp.exp(masked_scores(q_blk, k_blk, q_start, k_start, scale) - log_norm)
    dv_part = jnp.einsum('bhqk,bqhd->bkhd', attn_probs.astype(jnp.bfloat16), d_attn, preferred_element_type=jnp.float32)
    d_probs = jnp.einsum('bqhd,bkhd->bhqk', d_attn, v_blk, preferred_element_type=jnp.float32)
    d_scores = (attn_probs * (d_probs - delta) * scale).astype(jnp.bfloat16)
    dq_part = jnp.einsum('bhqk,bkhd->bqhd', d_scores, k_blk, preferred_element_type=jnp.float32)
    dk_part = jnp.einsum('bhqk,bqhd->bkhd', d_scores, q_blk, preferred_element_type=jnp.float32)
    return dq_part, dk_part, dv_part


def solution(mesh):
    cp_size = mesh.shape['cp']
    shift_perm = [(src_dev, (src_dev + 1) % cp_size) for src_dev in range(cp_size)]

    def device_fn(x_in, positions, long_factor, norm_gain, w_qkv, w_out, grad_y):
        batch, piece, hidden = x_in.shape
        head_dim = 2 * long_factor.shape[0]
        width = w_out.shape[0]
        heads = width // head_dim
        scale = 1.0 / math.sqrt(head_dim)
        my_index = lax.axis_index('cp')
        q_start = my_index * piece
        x_float = x_in.astype(jnp.float32)
        inv_rms = lax.rsqrt(jnp.mean(x_float * x_float, axis=-1, keepdims=True) + NORM_EPS)
        x_hat = x_float * inv_rms
        normed = (x_hat * norm_gain).astype(jnp.bfloat16)
        qkv_proj = jnp.einsum('bsd,de->bse', normed, w_qkv, preferred_element_type=jnp.float32)
        qkv_proj = qkv_proj.reshape(batch, piece, 3, heads, head_dim)
        cos_tab, sin_tab = rope_tables(positions, long_factor)
        q_rot = (qkv_proj[:, :, 0] * cos_tab + rotate_half(qkv_proj[:, :, 0]) * sin_tab).astype(jnp.bfloat16)
        k_rot = (qkv_proj[:, :, 1] * cos_tab + rotate_half(qkv_proj[:, :, 1]) * sin_tab).astype(jnp.bfloat16)
        v_val = qkv_proj[:, :, 2].astype(jnp.bfloat16)

        init_stats = (jnp.zeros((batch, piece, heads, head_dim), jnp.float32), jnp.full((batch, heads, piece, 1), MASK_VALUE, jnp.float32), jnp.zeros((batch, heads, piece, 1), jnp.float32))
        stats = fwd_block(init_stats, q_rot, k_rot, v_val, q_start, q_start, scale)

        def fwd_step(step_idx, state):
            stats, k_cur, v_cur = state
            k_cur = lax.ppermute(k_cur, 'cp', shift_perm)
            v_cur = lax.ppermute(v_cur, 'cp', shift_perm)
            k_start = (my_index - step_idx) * piece
            stats = lax.cond(step_idx <= my_index, lambda acc: fwd_block(acc, q_rot, k_cur, v_cur, q_start, k_start, scale), lambda acc: acc, stats)
            return stats, k_cur, v_cur

        stats, _, _ = lax.fori_loop(1, cp_size, fwd_step, (stats, k_rot, v_val))
        out_acc, row_max, row_sum = stats
        attn_out = (out_acc / jnp.transpose(row_sum, (0, 2, 1, 3))).astype(jnp.bfloat16)
        log_norm = row_max + jnp.log(row_sum)
        attn_flat = attn_out.reshape(batch, piece, width)
        y_out = (x_float + jnp.einsum('bsh,hd->bsd', attn_flat, w_out, preferred_element_type=jnp.float32)).astype(jnp.bfloat16)

        d_attn = jnp.einsum('bsd,hd->bsh', grad_y, w_out, preferred_element_type=jnp.float32).astype(jnp.bfloat16).reshape(batch, piece, heads, head_dim)
        g_wout = jnp.einsum('bsh,bsd->hd', attn_flat, grad_y, preferred_element_type=jnp.float32)
        delta = jnp.einsum('bqhd,bqhd->bhq', d_attn, attn_out, preferred_element_type=jnp.float32)[..., None]
        dq_acc, dk_own, dv_own = bwd_block(q_rot, k_rot, v_val, d_attn, log_norm, delta, q_start, q_start, scale)

        def bwd_step(step_idx, state):
            dq_acc, k_cur, v_cur, dk_cur, dv_cur = state
            k_cur = lax.ppermute(k_cur, 'cp', shift_perm)
            v_cur = lax.ppermute(v_cur, 'cp', shift_perm)
            dk_cur = lax.ppermute(dk_cur, 'cp', shift_perm)
            dv_cur = lax.ppermute(dv_cur, 'cp', shift_perm)
            k_start = (my_index - step_idx) * piece

            def add_block(sums):
                dq_sum, dk_sum, dv_sum = sums
                dq_part, dk_part, dv_part = bwd_block(q_rot, k_cur, v_cur, d_attn, log_norm, delta, q_start, k_start, scale)
                return dq_sum + dq_part, dk_sum + dk_part, dv_sum + dv_part

            dq_acc, dk_cur, dv_cur = lax.cond(step_idx <= my_index, add_block, lambda sums: sums, (dq_acc, dk_cur, dv_cur))
            return dq_acc, k_cur, v_cur, dk_cur, dv_cur

        dq_acc, _, _, dk_cur, dv_cur = lax.fori_loop(1, cp_size, bwd_step, (dq_acc, k_rot, v_val, dk_own, dv_own))
        dk_home = lax.ppermute(dk_cur, 'cp', shift_perm)
        dv_home = lax.ppermute(dv_cur, 'cp', shift_perm)

        dq_raw = dq_acc * cos_tab - rotate_half(dq_acc * sin_tab)
        dk_raw = dk_home * cos_tab - rotate_half(dk_home * sin_tab)
        d_qkv = jnp.stack([dq_raw.astype(jnp.bfloat16), dk_raw.astype(jnp.bfloat16), dv_home.astype(jnp.bfloat16)], axis=2).reshape(batch, piece, 3 * width)
        g_wqkv = jnp.einsum('bsd,bse->de', normed, d_qkv, preferred_element_type=jnp.float32)
        d_normed = jnp.einsum('bse,de->bsd', d_qkv, w_qkv, preferred_element_type=jnp.float32)
        g_gain = jnp.sum(d_normed * x_hat, axis=(0, 1))
        d_hat = d_normed * norm_gain
        dx_norm = inv_rms * (d_hat - x_hat * jnp.mean(d_hat * x_hat, axis=-1, keepdims=True))
        grad_x = (grad_y.astype(jnp.float32) + dx_norm).astype(jnp.bfloat16)
        g_gain, g_wqkv, g_wout = lax.psum((g_gain, g_wqkv, g_wout), 'cp')
        return y_out, grad_x, g_gain, g_wqkv, g_wout

    seq_spec = P('dp', 'cp', None)
    return jax.shard_map(device_fn, mesh=mesh, in_specs=(seq_spec, P(('dp', 'cp')), P(None), P(None), P(None, None), P(None, None), seq_spec), out_specs=(seq_spec, seq_spec, P('dp'), P('dp', None), P('dp', None)), check_vma=False)
```

profile of v0, /device:TPU:0, one launch (start us, length us, event | category | flops | bytes accessed | tf_op | source)
XLA Modules:
  0.0 5048.7 jit_solution(9655755934358705517)
XLA Ops:
  9.8 32.7 copy.23
  42.6 26.2 convolution_bitcast_fusion
  104.4 27.9 fusion.44
  132.3 24.3 fusion.41
  156.6 31.7 bitcast_add_fusion.5
  220.9 1054.8 %while.42 = (s32[]{:T(128)}, f32[1,768,32,64]{1,3,2,0:T(8,128)}, f32[1,32,768,1]{2,1,3,0:T(8,128)S(1)}, f32[1,32,768,1]{2,1,3,0:T(8,128)S(1)}, bf16[1,768,32,64]...) while((s32[]{:T(128)}, f32[1,768,32,64]{1,3,2,0:T(8,128)}, ...), condition=%wide.region_8.9_spmd, body=%wide.region_3.8_spmd.sunk | while | flops 5043267072 | bytes 292565376 | solution.py:89
  224.4 35.2 collective-permute-done
  259.6 33.7 collective-permute-done.1
  301.0 85.8 %collective-permute-start = (bf16[1,768,32,64]{1,3,2,0:T(8,128)(2,1)}, bf16[1,768,32,64]{1,3,2,0:T(8,128)(2,1)}, u32[]{:S(2)}, u32[]{:S(2)}) collective-permute-start(bf16[1,768,32,64]{1,3,2,0:T(8,128)(2,1)} %get-tuple-element.778), channel_id=1, source_target_pairs={{0,1},{1,2},{2,3},{3,4},{4,5},{5,6},{6,7},{7,0}} | collective-permute-start | bytes 9437192 | tf_op jit(solution)/shard_map/while/body/eval_jaxpr/ppermute | solution.py:83
  389.3 32.7 collective-permute-done
  422.0 33.7 collective-permute-done.1
  465.0 89.3 %collective-permute-start.1 = (bf16[1,768,32,64]{1,3,2,0:T(8,128)(2,1)}, bf16[1,768,32,64]{1,3,2,0:T(8,128)(2,1)}, u32[]{:S(2)}, u32[]{:S(2)}) collective-permute-start(bf16[1,768,32,64]{1,3,2,0:T(8,128)(2,1)} %get-tuple-element.779), channel_id=1, source_target_pairs={{0,1},{1,2},{2,3},{3,4},{4,5},{5,6},{6,7},{7,0}} | collective-permute-start | bytes 9437192 | tf_op jit(solution)/shard_map/while/body/eval_jaxpr/ppermute | solution.py:84
  554.3 30.2 collective-permute-done
  584.5 33.7 collective-permute-done.1
  632.4 114.5 %collective-permute-done = bf16[1,768,32,64]{1,3,2,0:T(8,128)(2,1)} collective-permute-done((bf16[1,768,32,64]{1,3,2,0:T(8,128)(2,1)}, bf16[1,768,32,64]{1,3,2,0:T(8,128)(2,1)}, u32[]{:S(2)}, u32[]{:S(2)}) %collective-permute-start) | collective-permute-done | bytes 3145760 | tf_op jit(solution)/shard_map/while/body/eval_jaxpr/ppermute | solution.py:83
  746.9 33.7 collective-permute-done.1
  788.4 121.0 %collective-permute-done = bf16[1,768,32,64]{1,3,2,0:T(8,128)(2,1)} collective-permute-done((bf16[1,768,32,64]{1,3,2,0:T(8,128)(2,1)}, bf16[1,768,32,64]{1,3,2,0:T(8,128)(2,1)}, u32[]{:S(2)}, u32[]{:S(2)}) %collective-permute-start) | collective-permute-done | bytes 3145760 | tf_op jit(solution)/shard_map/while/body/eval_jaxpr/ppermute | solution.py:83
  909.4 33.7 collective-permute-done.1
  950.8 121.0 %collective-permute-done = bf16[1,768,32,64]{1,3,2,0:T(8,128)(2,1)} collective-permute-done((bf16[1,768,32,64]{1,3,2,0:T(8,128)(2,1)}, bf16[1,768,32,64]{1,3,2,0:T(8,128)(2,1)}, u32[]{:S(2)}, u32[]{:S(2)}) %collective-permute-start) | collective-permute-done | bytes 3145760 | tf_op jit(solution)/shard_map/while/body/eval_jaxpr/ppermute | solution.py:83
  1071.8 33.7 collective-permute-done.1
  1113.3 121.0 %collective-permute-done = bf16[1,768,32,64]{1,3,2,0:T(8,128)(2,1)} collective-permute-done((bf16[1,768,32,64]{1,3,2,0:T(8,128)(2,1)}, bf16[1,768,32,64]{1,3,2,0:T(8,128)(2,1)}, u32[]{:S(2)}, u32[]{:S(2)}) %collective-permute-start) | collective-permute-done | bytes 3145760 | tf_op jit(solution)/shard_map/while/body/eval_jaxpr/ppermute | solution.py:83
  1234.3 33.7 collective-permute-done.1
  1275.8 31.1 fusion.85
  1313.0 43.4 multiply_convert_fusion.1
  1399.3 2553.2 %while.43 = (s32[]{:T(128)}, f32[1,768,32,64]{1,3,2,0:T(8,128)}, bf16[1,768,32,64]{1,3,2,0:T(8,128)(2,1)}, bf16[1,768,32,64]{1,3,2,0:T(8,128)(2,1)}, f32[1,768,3...) while((s32[]{:T(128)}, f32[1,768,32,64]{1,3,2,0:T(8,128)}, ...), condition=%wide.region_12.13_spmd, body=%wide.region_9.12_spmd.sunk | while | flops 12292524032 | bytes 514830816 | solution.py:117
  1399.9 255.7 %collective-permute-done.4 = bf16[1,768,32,64]{1,3,2,0:T(8,128)(2,1)} collective-permute-done((bf16[1,768,32,64]{1,3,2,0:T(8,128)(2,1)}, bf16[1,768,32,64]{1,3,2,0:T(8,128)(2,1)}, u32[]{:S(2)}, u32[]{:S(2)}) %collective-permute-start.4) | collective-permute-done | bytes 3145760 | tf_op jit(solution)/shard_map/while/body/eval_jaxpr/ppermute | solution.py:103
  1659.5 29.8 collective-permute-done.5
  1705.4 23.5 collective-permute-start.4
  1732.3 297.9 %collective-permute-done.4 = bf16[1,768,32,64]{1,3,2,0:T(8,128)(2,1)} collective-permute-done((bf16[1,768,32,64]{1,3,2,0:T(8,128)(2,1)}, bf16[1,768,32,64]{1,3,2,0:T(8,128)(2,1)}, u32[]{:S(2)}, u32[]{:S(2)}) %collective-permute-start.4) | collective-permute-done | bytes 3145760 | tf_op jit(solution)/shard_map/while/body/eval_jaxpr/ppermute | solution.py:103
  2034.0 29.8 collective-permute-done.5
  2079.9 26.9 collective-permute-start.4
  2110.2 294.5 %collective-permute-done.4 = bf16[1,768,32,64]{1,3,2,0:T(8,128)(2,1)} collective-permute-done((bf16[1,768,32,64]{1,3,2,0:T(8,128)(2,1)}, bf16[1,768,32,64]{1,3,2,0:T(8,128)(2,1)}, u32[]{:S(2)}, u32[]{:S(2)}) %collective-permute-start.4) | collective-permute-done | bytes 3145760 | tf_op jit(solution)/shard_map/while/body/eval_jaxpr/ppermute | solution.py:103
  2408.5 29.8 collective-permute-done.5
  2454.4 30.3 collective-permute-start.4
  2488.1 291.1 %collective-permute-done.4 = bf16[1,768,32,64]{1,3,2,0:T(8,128)(2,1)} collective-permute-done((bf16[1,768,32,64]{1,3,2,0:T(8,128)(2,1)}, bf16[1,768,32,64]{1,3,2,0:T(8,128)(2,1)}, u32[]{:S(2)}, u32[]{:S(2)}) %collective-permute-start.4) | collective-permute-done | bytes 3145760 | tf_op jit(solution)/shard_map/while/body/eval_jaxpr/ppermute | solution.py:103
  2783.0 29.8 collective-permute-done.5
  2828.9 37.1 collective-permute-start.5
  2866.0 287.6 %collective-permute-done.4 = bf16[1,768,32,64]{1,3,2,0:T(8,128)(2,1)} collective-permute-done((bf16[1,768,32,64]{1,3,2,0:T(8,128)(2,1)}, bf16[1,768,32,64]{1,3,2,0:T(8,128)(2,1)}, u32[]{:S(2)}, u32[]{:S(2)}) %collective-permute-start.4) | collective-permute-done | bytes 3145760 | tf_op jit(solution)/shard_map/while/body/eval_jaxpr/ppermute | solution.py:103
  3157.5 29.8 collective-permute-done.5
  3203.5 324.7 %collective-permute-done.4 = bf16[1,768,32,64]{1,3,2,0:T(8,128)(2,1)} collective-permute-done((bf16[1,768,32,64]{1,3,2,0:T(8,128)(2,1)}, bf16[1,768,32,64]{1,3,2,0:T(8,128)(2,1)}, u32[]{:S(2)}, u32[]{:S(2)}) %collective-permute-start.4) | collective-permute-done | bytes 3145760 | tf_op jit(solution)/shard_map/while/body/eval_jaxpr/ppermute | solution.py:103
  3532.0 29.8 collective-permute-done.5
  3578.0 324.7 %collective-permute-done.4 = bf16[1,768,32,64]{1,3,2,0:T(8,128)(2,1)} collective-permute-done((bf16[1,768,32,64]{1,3,2,0:T(8,128)(2,1)}, bf16[1,768,32,64]{1,3,2,0:T(8,128)(2,1)}, u32[]{:S(2)}, u32[]{:S(2)}) %collective-permute-start.4) | collective-permute-done | bytes 3145760 | tf_op jit(solution)/shard_map/while/body/eval_jaxpr/ppermute | solution.py:103
  3906.5 29.8 collective-permute-done.5
  3967.4 208.9 %collective-permute-done.6 = f32[1,768,32,64]{1,3,2,0:T(8,128)} collective-permute-done((f32[1,768,32,64]{1,3,2,0:T(8,128)}, f32[1,768,32,64]{1,3,2,0:T(8,128)}, u32[]{:S(2)}, u32[]{:S(2)}) %collective-permute-start.6) | collective-permute-done | bytes 6291488 | tf_op jit(solution)/shard_map/ppermute | solution.py:118
  4218.5 29.9 fusion.83
  4260.8 25.7 fusion.61
  4315.4 679.9 %all-reduce.3.cloned.1.call-done = (f32[2048,6144]{1,0:T(8,128)}, f32[2048,2048]{1,0:T(8,128)}) async-done(((f32[2048,6144]{1,0:T(8,128)}, f32[2048,2048]{1,0:T(8,128)}), (f32[2048,6144]{1,0:T(8,128)}, f32[2048,2048]{1,0:T(8,128)})) %all-reduce.3.cloned.1.call-update) | async-done | bytes 67108880 | tf_op jit(solution)/shard_map/psum | solution.py:130
  4995.3 34.5 copy.99
  (195 shorter events, 448.2 us)
Async XLA Ops:
  7.2 4988.2 %all-reduce.3.cloned.1.call-start = ((), (), s32[]{:S(2)}) async-start(), calls=%async_computation | async-start | bytes 134217728 | tf_op jit(solution)/shard_map/psum | solution.py:130
  9.8 32.8 copy-start.17
  9.8 32.8 copy-start.6
  220.9 38.6 collective-permute-start
  221.7 71.5 %collective-permute-start.1 = (bf16[1,768,32,64]{1,3,2,0:T(8,128)(2,1)}, bf16[1,768,32,64]{1,3,2,0:T(8,128)(2,1)}, u32[]{:S(2)}, u32[]{:S(2)}) collective-permute-start(bf16[1,768,32,64]{1,3,2,0:T(8,128)(2,1)} %get-tuple-element.779), channel_id=1, source_target_pairs={{0,1},{1,2},{2,3},{3,4},{4,5},{5,6},{6,7},{7,0}} | collective-permute-start | bytes 9437192 | tf_op jit(solution)/shard_map/while/body/eval_jaxpr/ppermute | solution.py:84
  301.0 121.0 %collective-permute-start = (bf16[1,768,32,64]{1,3,2,0:T(8,128)(2,1)}, bf16[1,768,32,64]{1,3,2,0:T(8,128)(2,1)}, u32[]{:S(2)}, u32[]{:S(2)}) collective-permute-start(bf16[1,768,32,64]{1,3,2,0:T(8,128)(2,1)} %get-tuple-element.778), channel_id=1, source_target_pairs={{0,1},{1,2},{2,3},{3,4},{4,5},{5,6},{6,7},{7,0}} | collective-permute-start | bytes 9437192 | tf_op jit(solution)/shard_map/while/body/eval_jaxpr/ppermute | solution.py:83
  386.8 68.9 %collective-permute-start.1 = (bf16[1,768,32,64]{1,3,2,0:T(8,128)(2,1)}, bf16[1,768,32,64]{1,3,2,0:T(8,128)(2,1)}, u32[]{:S(2)}, u32[]{:S(2)}) collective-permute-start(bf16[1,768,32,64]{1,3,2,0:T(8,128)(2,1)} %get-tuple-element.779), channel_id=1, source_target_pairs={{0,1},{1,2},{2,3},{3,4},{4,5},{5,6},{6,7},{7,0}} | collective-permute-start | bytes 9437192 | tf_op jit(solution)/shard_map/while/body/eval_jaxpr/ppermute | solution.py:84
  463.4 121.0 %collective-permute-start = (bf16[1,768,32,64]{1,3,2,0:T(8,128)(2,1)}, bf16[1,768,32,64]{1,3,2,0:T(8,128)(2,1)}, u32[]{:S(2)}, u32[]{:S(2)}) collective-permute-start(bf16[1,768,32,64]{1,3,2,0:T(8,128)(2,1)} %get-tuple-element.778), channel_id=1, source_target_pairs={{0,1},{1,2},{2,3},{3,4},{4,5},{5,6},{6,7},{7,0}} | collective-permute-start | bytes 9437192 | tf_op jit(solution)/shard_map/while/body/eval_jaxpr/ppermute | solution.py:83
  465.0 153.2 %collective-permute-start.1 = (bf16[1,768,32,64]{1,3,2,0:T(8,128)(2,1)}, bf16[1,768,32,64]{1,3,2,0:T(8,128)(2,1)}, u32[]{:S(2)}, u32[]{:S(2)}) collective-permute-start(bf16[1,768,32,64]{1,3,2,0:T(8,128)(2,1)} %get-tuple-element.779), channel_id=1, source_target_pairs={{0,1},{1,2},{2,3},{3,4},{4,5},{5,6},{6,7},{7,0}} | collective-permute-start | bytes 9437192 | tf_op jit(solution)/shard_map/while/body/eval_jaxpr/ppermute | solution.py:84
  625.9 121.0 %collective-permute-start = (bf16[1,768,32,64]{1,3,2,0:T(8,128)(2,1)}, bf16[1,768,32,64]{1,3,2,0:T(8,128)(2,1)}, u32[]{:S(2)}, u32[]{:S(2)}) collective-permute-start(bf16[1,768,32,64]{1,3,2,0:T(8,128)(2,1)} %get-tuple-element.778), channel_id=1, source_target_pairs={{0,1},{1,2},{2,3},{3,4},{4,5},{5,6},{6,7},{7,0}} | collective-permute-start | bytes 9437192 | tf_op jit(solution)/shard_map/while/body/eval_jaxpr/ppermute | solution.py:83
  629.9 150.7 %collective-permute-start.1 = (bf16[1,768,32,64]{1,3,2,0:T(8,128)(2,1)}, bf16[1,768,32,64]{1,3,2,0:T(8,128)(2,1)}, u32[]{:S(2)}, u32[]{:S(2)}) collective-permute-start(bf16[1,768,32,64]{1,3,2,0:T(8,128)(2,1)} %get-tuple-element.779), channel_id=1, source_target_pairs={{0,1},{1,2},{2,3},{3,4},{4,5},{5,6},{6,7},{7,0}} | collective-permute-start | bytes 9437192 | tf_op jit(solution)/shard_map/while/body/eval_jaxpr/ppermute | solution.py:84
  788.4 121.0 %collective-permute-start = (bf16[1,768,32,64]{1,3,2,0:T(8,128)(2,1)}, bf16[1,768,32,64]{1,3,2,0:T(8,128)(2,1)}, u32[]{:S(2)}, u32[]{:S(2)}) collective-permute-start(bf16[1,768,32,64]{1,3,2,0:T(8,128)(2,1)} %get-tuple-element.778), channel_id=1, source_target_pairs={{0,1},{1,2},{2,3},{3,4},{4,5},{5,6},{6,7},{7,0}} | collective-permute-start | bytes 9437192 | tf_op jit(solution)/shard_map/while/body/eval_jaxpr/ppermute | solution.py:83
  788.4 154.7 %collective-permute-start.1 = (bf16[1,768,32,64]{1,3,2,0:T(8,128)(2,1)}, bf16[1,768,32,64]{1,3,2,0:T(8,128)(2,1)}, u32[]{:S(2)}, u32[]{:S(2)}) collective-permute-start(bf16[1,768,32,64]{1,3,2,0:T(8,128)(2,1)} %get-tuple-element.779), channel_id=1, source_target_pairs={{0,1},{1,2},{2,3},{3,4},{4,5},{5,6},{6,7},{7,0}} | collective-permute-start | bytes 9437192 | tf_op jit(solution)/shard_map/while/body/eval_jaxpr/ppermute | solution.py:84
  950.8 121.0 %collective-permute-start = (bf16[1,768,32,64]{1,3,2,0:T(8,128)(2,1)}, bf16[1,768,32,64]{1,3,2,0:T(8,128)(2,1)}, u32[]{:S(2)}, u32[]{:S(2)}) collective-permute-start(bf16[1,768,32,64]{1,3,2,0:T(8,128)(2,1)} %get-tuple-element.778), channel_id=1, source_target_pairs={{0,1},{1,2},{2,3},{3,4},{4,5},{5,6},{6,7},{7,0}} | collective-permute-start | bytes 9437192 | tf_op jit(solution)/shard_map/while/body/eval_jaxpr/ppermute | solution.py:83
  950.8 154.7 %collective-permute-start.1 = (bf16[1,768,32,64]{1,3,2,0:T(8,128)(2,1)}, bf16[1,768,32,64]{1,3,2,0:T(8,128)(2,1)}, u32[]{:S(2)}, u32[]{:S(2)}) collective-permute-start(bf16[1,768,32,64]{1,3,2,0:T(8,128)(2,1)} %get-tuple-element.779), channel_id=1, source_target_pairs={{0,1},{1,2},{2,3},{3,4},{4,5},{5,6},{6,7},{7,0}} | collective-permute-start | bytes 9437192 | tf_op jit(solution)/shard_map/while/body/eval_jaxpr/ppermute | solution.py:84
  1113.3 121.0 %collective-permute-start = (bf16[1,768,32,64]{1,3,2,0:T(8,128)(2,1)}, bf16[1,768,32,64]{1,3,2,0:T(8,128)(2,1)}, u32[]{:S(2)}, u32[]{:S(2)}) collective-permute-start(bf16[1,768,32,64]{1,3,2,0:T(8,128)(2,1)} %get-tuple-element.778), channel_id=1, source_target_pairs={{0,1},{1,2},{2,3},{3,4},{4,5},{5,6},{6,7},{7,0}} | collective-permute-start | bytes 9437192 | tf_op jit(solution)/shard_map/while/body/eval_jaxpr/ppermute | solution.py:83
  1113.3 154.7 %collective-permute-start.1 = (bf16[1,768,32,64]{1,3,2,0:T(8,128)(2,1)}, bf16[1,768,32,64]{1,3,2,0:T(8,128)(2,1)}, u32[]{:S(2)}, u32[]{:S(2)}) collective-permute-start(bf16[1,768,32,64]{1,3,2,0:T(8,128)(2,1)} %get-tuple-element.779), channel_id=1, source_target_pairs={{0,1},{1,2},{2,3},{3,4},{4,5},{5,6},{6,7},{7,0}} | collective-permute-start | bytes 9437192 | tf_op jit(solution)/shard_map/while/body/eval_jaxpr/ppermute | solution.py:84
  1399.7 293.4 %collective-permute-start.2 = (f32[1,768,32,64]{1,3,2,0:T(8,128)}, f32[1,768,32,64]{1,3,2,0:T(8,128)}, u32[]{:S(2)}, u32[]{:S(2)}) collective-permute-start(f32[1,768,32,64]{1,3,2,0:T(8,128)} %get-tuple-element.811), channel_id=1, source_target_pairs={{0,1},{1,2},{2,3},{3,4},{4,5},{5,6},{6,7},{7,0}} | collective-permute-start | bytes 18874376 | tf_op jit(solution)/shard_map/while/body/eval_jaxpr/ppermute | solution.py:105
  1399.8 293.4 %collective-permute-start.3 = (f32[1,768,32,64]{1,3,2,0:T(8,128)}, f32[1,768,32,64]{1,3,2,0:T(8,128)}, u32[]{:S(2)}, u32[]{:S(2)}) collective-permute-start(f32[1,768,32,64]{1,3,2,0:T(8,128)} %get-tuple-element.812), channel_id=1, source_target_pairs={{0,1},{1,2},{2,3},{3,4},{4,5},{5,6},{6,7},{7,0}} | collective-permute-start | bytes 18874376 | tf_op jit(solution)/shard_map/while/body/eval_jaxpr/ppermute | solution.py:106
  1399.8 255.8 %collective-permute-start.4 = (bf16[1,768,32,64]{1,3,2,0:T(8,128)(2,1)}, bf16[1,768,32,64]{1,3,2,0:T(8,128)(2,1)}, u32[]{:S(2)}, u32[]{:S(2)}) collective-permute-start(bf16[1,768,32,64]{1,3,2,0:T(8,128)(2,1)} %get-tuple-element.809), channel_id=1, source_target_pairs={{0,1},{1,2},{2,3},{3,4},{4,5},{5,6},{6,7},{7,0}} | collective-permute-start | bytes 9437192 | tf_op jit(solution)/shard_map/while/body/eval_jaxpr/ppermute | solution.py:103
  1399.8 289.5 %collective-permute-start.5 = (bf16[1,768,32,64]{1,3,2,0:T(8,128)(2,1)}, bf16[1,768,32,64]{1,3,2,0:T(8,128)(2,1)}, u32[]{:S(2)}, u32[]{:S(2)}) collective-permute-start(bf16[1,768,32,64]{1,3,2,0:T(8,128)(2,1)} %get-tuple-element.810), channel_id=1, source_target_pairs={{0,1},{1,2},{2,3},{3,4},{4,5},{5,6},{6,7},{7,0}} | collective-permute-start | bytes 9437192 | tf_op jit(solution)/shard_map/while/body/eval_jaxpr/ppermute | solution.py:104
  1705.4 362.3 %collective-permute-start.2 = (f32[1,768,32,64]{1,3,2,0:T(8,128)}, f32[1,768,32,64]{1,3,2,0:T(8,128)}, u32[]{:S(2)}, u32[]{:S(2)}) collective-permute-start(f32[1,768,32,64]{1,3,2,0:T(8,128)} %get-tuple-element.811), channel_id=1, source_target_pairs={{0,1},{1,2},{2,3},{3,4},{4,5},{5,6},{6,7},{7,0}} | collective-permute-start | bytes 18874376 | tf_op jit(solution)/shard_map/while/body/eval_jaxpr/ppermute | solution.py:105
  1705.4 362.3 %collective-permute-start.3 = (f32[1,768,32,64]{1,3,2,0:T(8,128)}, f32[1,768,32,64]{1,3,2,0:T(8,128)}, u32[]{:S(2)}, u32[]{:S(2)}) collective-permute-start(f32[1,768,32,64]{1,3,2,0:T(8,128)} %get-tuple-element.812), channel_id=1, source_target_pairs={{0,1},{1,2},{2,3},{3,4},{4,5},{5,6},{6,7},{7,0}} | collective-permute-start | bytes 18874376 | tf_op jit(solution)/shard_map/while/body/eval_jaxpr/ppermute | solution.py:106
  1705.4 324.7 %collective-permute-start.4 = (bf16[1,768,32,64]{1,3,2,0:T(8,128)(2,1)}, bf16[1,768,32,64]{1,3,2,0:T(8,128)(2,1)}, u32[]{:S(2)}, u32[]{:S(2)}) collective-permute-start(bf16[1,768,32,64]{1,3,2,0:T(8,128)(2,1)} %get-tuple-element.809), channel_id=1, source_target_pairs={{0,1},{1,2},{2,3},{3,4},{4,5},{5,6},{6,7},{7,0}} | collective-permute-start | bytes 9437192 | tf_op jit(solution)/shard_map/while/body/eval_jaxpr/ppermute | solution.py:103
  1728.8 335.0 %collective-permute-start.5 = (bf16[1,768,32,64]{1,3,2,0:T(8,128)(2,1)}, bf16[1,768,32,64]{1,3,2,0:T(8,128)(2,1)}, u32[]{:S(2)}, u32[]{:S(2)}) collective-permute-start(bf16[1,768,32,64]{1,3,2,0:T(8,128)(2,1)} %get-tuple-element.810), channel_id=1, source_target_pairs={{0,1},{1,2},{2,3},{3,4},{4,5},{5,6},{6,7},{7,0}} | collective-permute-start | bytes 9437192 | tf_op jit(solution)/shard_map/while/body/eval_jaxpr/ppermute | solution.py:104
  2079.9 362.3 %collective-permute-start.2 = (f32[1,768,32,64]{1,3,2,0:T(8,128)}, f32[1,768,32,64]{1,3,2,0:T(8,128)}, u32[]{:S(2)}, u32[]{:S(2)}) collective-permute-start(f32[1,768,32,64]{1,3,2,0:T(8,128)} %get-tuple-element.811), channel_id=1, source_target_pairs={{0,1},{1,2},{2,3},{3,4},{4,5},{5,6},{6,7},{7,0}} | collective-permute-start | bytes 18874376 | tf_op jit(solution)/shard_map/while/body/eval_jaxpr/ppermute | solution.py:105
  2079.9 362.3 %collective-permute-start.3 = (f32[1,768,32,64]{1,3,2,0:T(8,128)}, f32[1,768,32,64]{1,3,2,0:T(8,128)}, u32[]{:S(2)}, u32[]{:S(2)}) collective-permute-start(f32[1,768,32,64]{1,3,2,0:T(8,128)} %get-tuple-element.812), channel_id=1, source_target_pairs={{0,1},{1,2},{2,3},{3,4},{4,5},{5,6},{6,7},{7,0}} | collective-permute-start | bytes 18874376 | tf_op jit(solution)/shard_map/while/body/eval_jaxpr/ppermute | solution.py:106
  2079.9 324.7 %collective-permute-start.4 = (bf16[1,768,32,64]{1,3,2,0:T(8,128)(2,1)}, bf16[1,768,32,64]{1,3,2,0:T(8,128)(2,1)}, u32[]{:S(2)}, u32[]{:S(2)}) collective-permute-start(bf16[1,768,32,64]{1,3,2,0:T(8,128)(2,1)} %get-tuple-element.809), channel_id=1, source_target_pairs={{0,1},{1,2},{2,3},{3,4},{4,5},{5,6},{6,7},{7,0}} | collective-permute-start | bytes 9437192 | tf_op jit(solution)/shard_map/while/body/eval_jaxpr/ppermute | solution.py:103
  2106.8 331.6 %collective-permute-start.5 = (bf16[1,768,32,64]{1,3,2,0:T(8,128)(2,1)}, bf16[1,768,32,64]{1,3,2,0:T(8,128)(2,1)}, u32[]{:S(2)}, u32[]{:S(2)}) collective-permute-start(bf16[1,768,32,64]{1,3,2,0:T(8,128)(2,1)} %get-tuple-element.810), channel_id=1, source_target_pairs={{0,1},{1,2},{2,3},{3,4},{4,5},{5,6},{6,7},{7,0}} | collective-permute-start | bytes 9437192 | tf_op jit(solution)/shard_map/while/body/eval_jaxpr/ppermute | solution.py:104
  2454.4 362.3 %collective-permute-start.2 = (f32[1,768,32,64]{1,3,2,0:T(8,128)}, f32[1,768,32,64]{1,3,2,0:T(8,128)}, u32[]{:S(2)}, u32[]{:S(2)}) collective-permute-start(f32[1,768,32,64]{1,3,2,0:T(8,128)} %get-tuple-element.811), channel_id=1, source_target_pairs={{0,1},{1,2},{2,3},{3,4},{4,5},{5,6},{6,7},{7,0}} | collective-permute-start | bytes 18874376 | tf_op jit(solution)/shard_map/while/body/eval_jaxpr/ppermute | solution.py:105
  2454.4 362.3 %collective-permute-start.3 = (f32[1,768,32,64]{1,3,2,0:T(8,128)}, f32[1,768,32,64]{1,3,2,0:T(8,128)}, u32[]{:S(2)}, u32[]{:S(2)}) collective-permute-start(f32[1,768,32,64]{1,3,2,0:T(8,128)} %get-tuple-element.812), channel_id=1, source_target_pairs={{0,1},{1,2},{2,3},{3,4},{4,5},{5,6},{6,7},{7,0}} | collective-permute-start | bytes 18874376 | tf_op jit(solution)/shard_map/while/body/eval_jaxpr/ppermute | solution.py:106
  2454.4 324.7 %collective-permute-start.4 = (bf16[1,768,32,64]{1,3,2,0:T(8,128)(2,1)}, bf16[1,768,32,64]{1,3,2,0:T(8,128)(2,1)}, u32[]{:S(2)}, u32[]{:S(2)}) collective-permute-start(bf16[1,768,32,64]{1,3,2,0:T(8,128)(2,1)} %get-tuple-element.809), channel_id=1, source_target_pairs={{0,1},{1,2},{2,3},{3,4},{4,5},{5,6},{6,7},{7,0}} | collective-permute-start | bytes 9437192 | tf_op jit(solution)/shard_map/while/body/eval_jaxpr/ppermute | solution.py:103
  2484.7 328.2 %collective-permute-start.5 = (bf16[1,768,32,64]{1,3,2,0:T(8,128)(2,1)}, bf16[1,768,32,64]{1,3,2,0:T(8,128)(2,1)}, u32[]{:S(2)}, u32[]{:S(2)}) collective-permute-start(bf16[1,768,32,64]{1,3,2,0:T(8,128)(2,1)} %get-tuple-element.810), channel_id=1, source_target_pairs={{0,1},{1,2},{2,3},{3,4},{4,5},{5,6},{6,7},{7,0}} | collective-permute-start | bytes 9437192 | tf_op jit(solution)/shard_map/while/body/eval_jaxpr/ppermute | solution.py:104
  2828.9 362.3 %collective-permute-start.2 = (f32[1,768,32,64]{1,3,2,0:T(8,128)}, f32[1,768,32,64]{1,3,2,0:T(8,128)}, u32[]{:S(2)}, u32[]{:S(2)}) collective-permute-start(f32[1,768,32,64]{1,3,2,0:T(8,128)} %get-tuple-element.811), channel_id=1, source_target_pairs={{0,1},{1,2},{2,3},{3,4},{4,5},{5,6},{6,7},{7,0}} | collective-permute-start | bytes 18874376 | tf_op jit(solution)/shard_map/while/body/eval_jaxpr/ppermute | solution.py:105
  2828.9 362.3 %collective-permute-start.3 = (f32[1,768,32,64]{1,3,2,0:T(8,128)}, f32[1,768,32,64]{1,3,2,0:T(8,128)}, u32[]{:S(2)}, u32[]{:S(2)}) collective-permute-start(f32[1,768,32,64]{1,3,2,0:T(8,128)} %get-tuple-element.812), channel_id=1, source_target_pairs={{0,1},{1,2},{2,3},{3,4},{4,5},{5,6},{6,7},{7,0}} | collective-permute-start | bytes 18874376 | tf_op jit(solution)/shard_map/while/body/eval_jaxpr/ppermute | solution.py:106
  2828.9 324.7 %collective-permute-start.4 = (bf16[1,768,32,64]{1,3,2,0:T(8,128)(2,1)}, bf16[1,768,32,64]{1,3,2,0:T(8,128)(2,1)}, u32[]{:S(2)}, u32[]{:S(2)}) collective-permute-start(bf16[1,768,32,64]{1,3,2,0:T(8,128)(2,1)} %get-tuple-element.809), channel_id=1, source_target_pairs={{0,1},{1,2},{2,3},{3,4},{4,5},{5,6},{6,7},{7,0}} | collective-permute-start | bytes 9437192 | tf_op jit(solution)/shard_map/while/body/eval_jaxpr/ppermute | solution.py:103
  2828.9 358.4 %collective-permute-start.5 = (bf16[1,768,32,64]{1,3,2,0:T(8,128)(2,1)}, bf16[1,768,32,64]{1,3,2,0:T(8,128)(2,1)}, u32[]{:S(2)}, u32[]{:S(2)}) collective-permute-start(bf16[1,768,32,64]{1,3,2,0:T(8,128)(2,1)} %get-tuple-element.810), channel_id=1, source_target_pairs={{0,1},{1,2},{2,3},{3,4},{4,5},{5,6},{6,7},{7,0}} | collective-permute-start | bytes 9437192 | tf_op jit(solution)/shard_map/while/body/eval_jaxpr/ppermute | solution.py:104
  3203.4 362.3 %collective-permute-start.2 = (f32[1,768,32,64]{1,3,2,0:T(8,128)}, f32[1,768,32,64]{1,3,2,0:T(8,128)}, u32[]{:S(2)}, u32[]{:S(2)}) collective-permute-start(f32[1,768,32,64]{1,3,2,0:T(8,128)} %get-tuple-element.811), channel_id=1, source_target_pairs={{0,1},{1,2},{2,3},{3,4},{4,5},{5,6},{6,7},{7,0}} | collective-permute-start | bytes 18874376 | tf_op jit(solution)/shard_map/while/body/eval_jaxpr/ppermute | solution.py:105
  3203.4 362.3 %collective-permute-start.3 = (f32[1,768,32,64]{1,3,2,0:T(8,128)}, f32[1,768,32,64]{1,3,2,0:T(8,128)}, u32[]{:S(2)}, u32[]{:S(2)}) collective-permute-start(f32[1,768,32,64]{1,3,2,0:T(8,128)} %get-tuple-element.812), channel_id=1, source_target_pairs={{0,1},{1,2},{2,3},{3,4},{4,5},{5,6},{6,7},{7,0}} | collective-permute-start | bytes 18874376 | tf_op jit(solution)/shard_map/while/body/eval_jaxpr/ppermute | solution.py:106
  3203.4 324.7 %collective-permute-start.4 = (bf16[1,768,32,64]{1,3,2,0:T(8,128)(2,1)}, bf16[1,768,32,64]{1,3,2,0:T(8,128)(2,1)}, u32[]{:S(2)}, u32[]{:S(2)}) collective-permute-start(bf16[1,768,32,64]{1,3,2,0:T(8,128)(2,1)} %get-tuple-element.809), channel_id=1, source_target_pairs={{0,1},{1,2},{2,3},{3,4},{4,5},{5,6},{6,7},{7,0}} | collective-permute-start | bytes 9437192 | tf_op jit(solution)/shard_map/while/body/eval_jaxpr/ppermute | solution.py:103
  3203.4 358.4 %collective-permute-start.5 = (bf16[1,768,32,64]{1,3,2,0:T(8,128)(2,1)}, bf16[1,768,32,64]{1,3,2,0:T(8,128)(2,1)}, u32[]{:S(2)}, u32[]{:S(2)}) collective-permute-start(bf16[1,768,32,64]{1,3,2,0:T(8,128)(2,1)} %get-tuple-element.810), channel_id=1, source_target_pairs={{0,1},{1,2},{2,3},{3,4},{4,5},{5,6},{6,7},{7,0}} | collective-permute-start | bytes 9437192 | tf_op jit(solution)/shard_map/while/body/eval_jaxpr/ppermute | solution.py:104
  3577.9 362.3 %collective-permute-start.2 = (f32[1,768,32,64]{1,3,2,0:T(8,128)}, f32[1,768,32,64]{1,3,2,0:T(8,128)}, u32[]{:S(2)}, u32[]{:S(2)}) collective-permute-start(f32[1,768,32,64]{1,3,2,0:T(8,128)} %get-tuple-element.811), channel_id=1, source_target_pairs={{0,1},{1,2},{2,3},{3,4},{4,5},{5,6},{6,7},{7,0}} | collective-permute-start | bytes 18874376 | tf_op jit(solution)/shard_map/while/body/eval_jaxpr/ppermute | solution.py:105
  3577.9 362.3 %collective-permute-start.3 = (f32[1,768,32,64]{1,3,2,0:T(8,128)}, f32[1,768,32,64]{1,3,2,0:T(8,128)}, u32[]{:S(2)}, u32[]{:S(2)}) collective-permute-start(f32[1,768,32,64]{1,3,2,0:T(8,128)} %get-tuple-element.812), channel_id=1, source_target_pairs={{0,1},{1,2},{2,3},{3,4},{4,5},{5,6},{6,7},{7,0}} | collective-permute-start | bytes 18874376 | tf_op jit(solution)/shard_map/while/body/eval_jaxpr/ppermute | solution.py:106
  3577.9 324.7 %collective-permute-start.4 = (bf16[1,768,32,64]{1,3,2,0:T(8,128)(2,1)}, bf16[1,768,32,64]{1,3,2,0:T(8,128)(2,1)}, u32[]{:S(2)}, u32[]{:S(2)}) collective-permute-start(bf16[1,768,32,64]{1,3,2,0:T(8,128)(2,1)} %get-tuple-element.809), channel_id=1, source_target_pairs={{0,1},{1,2},{2,3},{3,4},{4,5},{5,6},{6,7},{7,0}} | collective-permute-start | bytes 9437192 | tf_op jit(solution)/shard_map/while/body/eval_jaxpr/ppermute | solution.py:103
  3577.9 358.4 %collective-permute-start.5 = (bf16[1,768,32,64]{1,3,2,0:T(8,128)(2,1)}, bf16[1,768,32,64]{1,3,2,0:T(8,128)(2,1)}, u32[]{:S(2)}, u32[]{:S(2)}) collective-permute-start(bf16[1,768,32,64]{1,3,2,0:T(8,128)(2,1)} %get-tuple-element.810), channel_id=1, source_target_pairs={{0,1},{1,2},{2,3},{3,4},{4,5},{5,6},{6,7},{7,0}} | collective-permute-start | bytes 9437192 | tf_op jit(solution)/shard_map/while/body/eval_jaxpr/ppermute | solution.py:104
  3952.6 223.6 %collective-permute-start.6 = (f32[1,768,32,64]{1,3,2,0:T(8,128)}, f32[1,768,32,64]{1,3,2,0:T(8,128)}, u32[]{:S(2)}, u32[]{:S(2)}) collective-permute-start(f32[1,768,32,64]{1,3,2,0:T(8,128)} %get-tuple-element.507), channel_id=1, source_target_pairs={{0,1},{1,2},{2,3},{3,4},{4,5},{5,6},{6,7},{7,0}} | collective-permute-start | bytes 18874376 | tf_op jit(solution)/shard_map/ppermute | solution.py:118
  3957.7 252.3 %collective-permute-start.7 = (bf16[1,768,32,64]{1,3,2,0:T(8,128)(2,1)}, bf16[1,768,32,64]{1,3,2,0:T(8,128)(2,1)}, u32[]{:S(2)}, u32[]{:S(2)}) collective-permute-start(bf16[1,768,32,64]{1,3,2,0:T(8,128)(2,1)} %convert.15), channel_id=1, source_target_pairs={{0,1},{1,2},{2,3},{3,4},{4,5},{5,6},{6,7},{7,0}} | collective-permute-start | bytes 9437192 | tf_op jit(solution)/shard_map/ppermute | solution.py:119
  3957.8 218.5 %copy-start.14 = (f32[768,64]{0,1:T(8,128)S(1)}, f32[768,64]{0,1:T(8,128)}, u32[]{:S(2)}) copy-start(f32[768,64]{0,1:T(8,128)} %copy-done.13) | copy-start | bytes 589828
  (21 other events, 247.9 us)
Sparse Core Ops, SparseCore 0:
  4248.6 746.7 all-reduce.2
where the time goes:
time: 5060 us; the launch traced here: 5050 us
  waiting for transfers between devices  3990 us (79%)
  starting transfers between devices  317 us (6%)
  local copies, waits for them, and re-layouts  301 us (6%)
  matrix products  293 us (6%)
  other arithmetic  106 us (2%)
    ppermute x7, waiting for transfers between devices, bwd_step(): k_cur = lax.ppermute(k_cur, 'cp', shift_perm)  2080 us
    psum x1, waiting for transfers between devices, device_fn(): g_gain, g_wqkv, g_wout = lax.psum((g_gain, g_wqkv, g_wout), 'cp')  680 us
    ppermute x7, waiting for transfers between devices, fwd_step(): k_cur = lax.ppermute(k_cur, 'cp', shift_perm)  576 us
    ppermute x7, waiting for transfers between devices, fwd_step(): v_cur = lax.ppermute(v_cur, 'cp', shift_perm)  236 us
    ppermute x1, waiting for transfers between devices, device_fn(): dk_home = lax.ppermute(dk_cur, 'cp', shift_perm)  209 us
    ppermute x7, waiting for transfers between devices, bwd_step(): v_cur = lax.ppermute(v_cur, 'cp', shift_perm)  209 us
    while x42, local copies, waits for them, and re-layouts  194 us
  transfers between devices with their start and end apart: 45, of which 31 were waited for; matrix products, arithmetic and copies ran while one was open for 3% of the time, Pallas kernels for 0%

commit v1 on v0

v1 whole, which is shorter than its diff:
```python
import math
import jax
import jax.numpy as jnp
from jax import lax
from jax.experimental import pallas as pl
from jax.experimental.pallas import tpu as pltpu
from jax.sharding import PartitionSpec as P

NORM_EPS = 1e-5
MSCALE = math.sqrt(1.0 + math.log(32.0) / math.log(4096.0))
MASK_VALUE = -1e30
LOG2E = math.log2(math.e)
BF16 = jnp.bfloat16
F32 = jnp.float32
BLK = 512
VMEM_LIMIT = 60 * 1024 * 1024


def dot_nn(a, b):
    return lax.dot_general(a, b, (((1,), (0,)), ((), ())), preferred_element_type=F32)


def dot_nt(a, b):
    return lax.dot_general(a, b, (((1,), (1,)), ((), ())), preferred_element_type=F32)


def params(n=1, **kw):
    return pltpu.CompilerParams(dimension_semantics=("arbitrary",) * n, vmem_limit_bytes=VMEM_LIMIT, **kw)


def cost(flops, nbytes, trans=0):
    return pl.CostEstimate(flops=int(flops), bytes_accessed=int(nbytes), transcendentals=int(trans))


def qkv_kernel(d_ref, r_ref, wq_ref, wk_ref, wv_ref, cos_ref, sin_ref, q_out, k_out, v_out, kn_out, w_scr):
    width = wq_ref.shape[1]

    @pl.when(pl.program_id(0) == 0)
    def _():
        w_scr[0:width] = wq_ref[...].T
        w_scr[width:2 * width] = wk_ref[...].T
        w_scr[2 * width:] = wv_ref[...].T

    cos = cos_ref[...]
    sin = sin_ref[...]
    r_blk = r_ref[...]
    half = cos.shape[0]

    def rope(t):
        rows = []
        for h in range(width // (2 * half)):
            t1 = t[2 * half * h:2 * half * h + half]
            t2 = t[2 * half * h + half:2 * half * (h + 1)]
            rows += [t1 * cos - t2 * sin, t2 * cos + t1 * sin]
        return jnp.concatenate(rows, axis=0).astype(BF16)

    q_out[...] = rope(dot_nt(w_scr[0:width], r_blk)) * BF16(0.125)
    k_rot = rope(dot_nt(w_scr[width:2 * width], r_blk))
    k_out[...] = k_rot
    kn_out[...] = k_rot.T
    v_out[...] = dot_nt(w_scr[2 * width:], r_blk).astype(BF16)


def qkv_call(dev, r_all, w_qkv, cos_t, sin_t):
    seq, hidden = r_all.shape
    width = 256
    ndev = w_qkv.shape[1] // (3 * width)
    half = cos_t.shape[0]
    tr = jax.ShapeDtypeStruct((width, seq), BF16)
    wspec = lambda which: pl.BlockSpec((hidden, width), lambda i, d: (0, which * ndev + d[0]))
    tspec = pl.BlockSpec((width, BLK), lambda i, d: (0, i))
    return pl.pallas_call(
        qkv_kernel,
        out_shape=(tr, tr, tr, jax.ShapeDtypeStruct((seq, width), BF16)),
        grid_spec=pltpu.PrefetchScalarGridSpec(
            num_scalar_prefetch=1,
            grid=(seq // BLK,),
            in_specs=[
                pl.BlockSpec((BLK, hidden), lambda i, d: (i, 0)),
                wspec(0), wspec(1), wspec(2),
                pl.BlockSpec((half, BLK), lambda i, d: (0, i)),
                pl.BlockSpec((half, BLK), lambda i, d: (0, i)),
            ],
            out_specs=(tspec, tspec, tspec, pl.BlockSpec((BLK, width), lambda i, d: (i, 0))),
            scratch_shapes=[pltpu.VMEM((3 * width, hidden), BF16)],
        ),
        compiler_params=params(1),
        cost_estimate=cost(2 * seq * hidden * 3 * width, seq * hidden * 2 + seq * width * 8),
        name="qkv",
    )(dev, r_all, w_qkv, w_qkv, w_qkv, cos_t, sin_t)


def fwd_kernel(q_ref, k_ref, v_ref, o_out, on_out, lse_out, qz_scr, acc_scr, m_scr, l_scr):
    i = pl.program_id(1)
    q_blk = q_ref[...]
    zero = jnp.zeros((64, BLK), BF16)
    qz_scr[0] = jnp.concatenate([q_blk[0:64], zero], axis=0)
    qz_scr[1] = jnp.concatenate([zero, q_blk[64:128]], axis=0)
    acc_scr[...] = jnp.zeros_like(acc_scr)
    m_scr[...] = jnp.full_like(m_scr, MASK_VALUE)
    l_scr[...] = jnp.zeros_like(l_scr)

    def step(j, masked):
        off = pl.multiple_of(j * BLK, BLK)
        k_blk = k_ref[pl.ds(off, BLK), :]
        scores = [dot_nn(k_blk, qz_scr[h]) * LOG2E for h in range(2)]
        for h in range(2):
            s = scores[h]
            if masked:
                krow = lax.broadcasted_iota(jnp.int32, s.shape, 0)
                qcol = lax.broadcasted_iota(jnp.int32, s.shape, 1)
                s = jnp.where(krow <= qcol, s, MASK_VALUE)
            m_old = m_scr[h:h + 1, :]
            m_new = jnp.maximum(m_old, jnp.max(s, axis=0, keepdims=True))
            m_scr[h:h + 1, :] = m_new
            alpha = jnp.exp2(m_old - m_new)
            p = jnp.exp2(s - m_new)
            l_scr[h:h + 1, :] = l_scr[h:h + 1, :] * alpha + jnp.sum(p, axis=0, keepdims=True)
            pv = dot_nn(v_ref[64 * h:64 * h + 64, pl.ds(off, BLK)], p.astype(BF16))
            acc_scr[h] = acc_scr[h] * alpha + pv

    def body(j, carry):
        step(j, False)
        return carry

    lax.fori_loop(0, i, body, 0)
    step(i, True)
    outs = []
    for h in range(2):
        l = l_scr[h:h + 1, :]
        outs.append((acc_scr[h] / l).astype(BF16))
        lse_out[h:h + 1, :] = m_scr[h:h + 1, :] * (1.0 / LOG2E) + jnp.log(l)
    o_blk = jnp.concatenate(outs, axis=0)
    o_out[...] = o_blk
    on_out[...] = o_blk.T


def fwd_call(q_t, k_n, v_t):
    width, seq = q_t.shape
    pairs = width // 128
    nblk = seq // BLK
    return pl.pallas_call(
        fwd_kernel,
        out_shape=(jax.ShapeDtypeStruct((width, seq), BF16), jax.ShapeDtypeStruct((seq, width), BF16), jax.ShapeDtypeStruct((8 * pairs, seq), F32)),
        grid=(pairs, nblk),
        in_specs=[
            pl.BlockSpec((128, BLK), lambda p, i: (p, i)),
            pl.BlockSpec((seq, 128), lambda p, i: (0, p)),
            pl.BlockSpec((128, seq), lambda p, i: (p, 0)),
        ],
        out_specs=(
            pl.BlockSpec((128, BLK), lambda p, i: (p, i)),
            pl.BlockSpec((BLK, 128), lambda p, i: (i, p)),
            pl.BlockSpec((8, BLK), lambda p, i: (p, i)),
        ),
        scratch_shapes=[pltpu.VMEM((2, 128, BLK), BF16), pltpu.VMEM((2, 64, BLK), F32), pltpu.VMEM((8, BLK), F32), pltpu.VMEM((8, BLK), F32)],
        compiler_params=params(2),
        cost_estimate=cost(2 * 2 * seq * seq * width * 2, seq * width * 10, seq * seq),
        name="attn_fwd",
    )(q_t, k_n, v_t)


def y_kernel(o_ref, w_ref, x_ref, y_out, acc_scr):
    s = pl.program_id(0)
    part = dot_nn(o_ref[0], w_ref[...])

    @pl.when(s == 0)
    def _():
        acc_scr[...] = part

    @pl.when(s > 0)
    def _():
        acc_scr[...] += part

    @pl.when(s == pl.num_programs(0) - 1)
    def _():
        y_out[...] = (x_ref[...].astype(F32) + acc_scr[...]).astype(BF16)


def y_call(o_parts, w_out, x):
    ndev, piece, width = o_parts.shape
    hidden = w_out.shape[1]
    return pl.pallas_call(
        y_kernel,
        out_shape=jax.ShapeDtypeStruct((piece, hidden), BF16),
        grid=(ndev,),
        in_specs=[
            pl.BlockSpec((1, piece, width), lambda s: (s, 0, 0)),
            pl.BlockSpec((width, hidden), lambda s: (s, 0)),
            pl.BlockSpec((piece, hidden), lambda s: (0, 0)),
        ],
        out_specs=pl.BlockSpec((piece, hidden), lambda s: (0, 0)),
        scratch_shapes=[pltpu.VMEM((piece, hidden), F32)],
        compiler_params=params(1),
        cost_estimate=cost(2 * piece * hidden * ndev * width, 20e6),
        name="y_proj",
    )(o_parts, w_out, x)


def do_kernel(d_ref, dy_ref, w_ref, o_ref, do_out, gw_out):
    dy = dy_ref[...]
    do_out[...] = dot_nt(w_ref[...], dy).astype(BF16)
    part = dot_nn(o_ref[...], dy)

    @pl.when(pl.program_id(0) == 0)
    def _():
        gw_out[...] = part

    @pl.when(pl.program_id(0) > 0)
    def _():
        gw_out[...] += part


def do_call(dev, dy_all, w_out, o_t):
    seq, hidden = dy_all.shape
    width = o_t.shape[0]
    return pl.pallas_call(
        do_kernel,
        out_shape=(jax.ShapeDtypeStruct((width, seq), BF16), jax.ShapeDtypeStruct((width, hidden), F32)),
        grid_spec=pltpu.PrefetchScalarGridSpec(
            num_scalar_prefetch=1,
            grid=(seq // BLK,),
            in_specs=[
                pl.BlockSpec((BLK, hidden), lambda i, d: (i, 0)),
                pl.BlockSpec((width, hidden), lambda i, d: (d[0], 0)),
                pl.BlockSpec((width, BLK), lambda i, d: (0, i)),
            ],
            out_specs=(pl.BlockSpec((width, BLK), lambda i, d: (0, i)), pl.BlockSpec((width, hidden), lambda i, d: (0, 0))),
        ),
        compiler_params=params(1),
        cost_estimate=cost(4 * seq * hidden * width, seq * hidden * 2),
        name="do_gwout",
    )(dev, dy_all, w_out, o_t)


def split3(value):
    hi = value.astype(BF16).astype(F32)
    mid = (value - hi).astype(BF16).astype(F32)
    return hi, mid, value - hi - mid


def bwd_kernel(q_ref, do_ref, o_ref, lse_ref, k_ref, v_ref, cos_ref, sin_ref, dq_out, dk_out, dv_out, dn_out, qa_scr, doa_scr, ka_scr, va_scr, dq_scr, dk_scr, dv_scr):
    j = pl.program_id(0)
    nblk = pl.num_programs(0)
    row64 = lax.broadcasted_iota(jnp.int32, (64, BLK), 0)

    def augment(data, stat):
        hi, mid, lo = split3(-stat)
        extra = jnp.where(row64 == 0, hi, jnp.where(row64 == 1, mid, jnp.where(row64 == 2, lo, 0.0))).astype(BF16)
        return jnp.concatenate([data, extra], axis=0).T

    @pl.when(j == 0)
    def _():
        dq_scr[...] = jnp.zeros_like(dq_scr)

        def prep(t, carry):
            cols = pl.ds(pl.multiple_of(t * BLK, BLK), BLK)
            for h in range(2):
                rows = slice(64 * h, 64 * h + 64)
                do_h = do_ref[rows, cols]
                delta = jnp.sum(do_h.astype(F32) * o_ref[rows, cols].astype(F32), axis=0, keepdims=True)
                qa_scr[h, cols, :] = augment(q_ref[rows, cols], lse_ref[h:h + 1, cols])
                doa_scr[h, cols, :] = augment(do_h, delta)
            return carry

        lax.fori_loop(0, nblk, prep, 0)

    ones = jnp.where(row64 < 3, 1.0, 0.0).astype(BF16)
    for h in range(2):
        rows = slice(64 * h, 64 * h + 64)
        ka_scr[h] = jnp.concatenate([k_ref[rows, :], ones], axis=0)
        va_scr[h] = jnp.concatenate([v_ref[rows, :], ones], axis=0)
    dk_scr[...] = jnp.zeros_like(dk_scr)
    dv_scr[...] = jnp.zeros_like(dv_scr)

    def step(i, masked):
        cols = pl.ds(pl.multiple_of(i * BLK, BLK), BLK)
        for h in range(2):
            rows = slice(64 * h, 64 * h + 64)
            s = dot_nn(qa_scr[h, cols, :], ka_scr[h])
            if masked:
                qrow = lax.broadcasted_iota(jnp.int32, s.shape, 0)
                kcol = lax.broadcasted_iota(jnp.int32, s.shape, 1)
                s = jnp.where(kcol <= qrow, s, MASK_VALUE)
            p = jnp.exp2(s * LOG2E)
            dp = dot_nn(doa_scr[h, cols, :], va_scr[h])
            ds = (p * dp).astype(BF16)
            dv_scr[h] += dot_nn(do_ref[rows, cols], p.astype(BF16))
            dk_scr[h] += dot_nn(q_ref[rows, cols], ds)
            dq_scr[rows, cols] += dot_nt(k_ref[rows, :], ds)

    def body(i, carry):
        step(i, False)
        return carry

    step(j, True)
    lax.fori_loop(j + 1, nblk, body, 0)

    cos = cos_ref[...]
    sin = sin_ref[...]

    def unrope(t, scale):
        t1 = t[0:32] * scale
        t2 = t[32:64] * scale
        return jnp.concatenate([t1 * cos + t2 * sin, t2 * cos - t1 * sin], axis=0).astype(BF16)

    own = pl.ds(pl.multiple_of(j * BLK, BLK), BLK)
    dq = jnp.concatenate([unrope(dq_scr[64 * h:64 * h + 64, own], 0.125) for h in range(2)], axis=0)
    dk = jnp.concatenate([unrope(dk_scr[h], 1.0) for h in range(2)], axis=0)
    dv = jnp.concatenate([dv_scr[h].astype(BF16) for h in range(2)], axis=0)
    dq_out[...] = dq
    dk_out[...] = dk
    dv_out[...] = dv
    dn_out[:, 0:128] = dq.T
    dn_out[:, 128:256] = dk.T
    dn_out[:, 256:384] = dv.T


def bwd_call(p, q_t, do_t, o_t, lse, k_t, v_t, cos_t, sin_t):
    seq = q_t.shape[1]
    half = cos_t.shape[0]
    full = pl.BlockSpec((128, seq), lambda j: (p, 0))
    blk = pl.BlockSpec((128, BLK), lambda j: (p, j))
    tab = pl.BlockSpec((half, BLK), lambda j: (0, j))
    tr = jax.ShapeDtypeStruct((128, seq), BF16)
    trs = pl.BlockSpec((128, BLK), lambda j: (0, j))
    return pl.pallas_call(
        bwd_kernel,
        out_shape=(tr, tr, tr, jax.ShapeDtypeStruct((seq, 384), BF16)),
        grid=(seq // BLK,),
        in_specs=[full, full, full, pl.BlockSpec((8, seq), lambda j: (p, 0)), blk, blk, tab, tab],
        out_specs=(trs, trs, trs, pl.BlockSpec((BLK, 384), lambda j: (j, 0))),
        scratch_shapes=[
            pltpu.VMEM((2, seq, 128), BF16), pltpu.VMEM((2, seq, 128), BF16),
            pltpu.VMEM((2, 128, BLK), BF16), pltpu.VMEM((2, 128, BLK), BF16),
            pltpu.VMEM((128, seq), F32), pltpu.VMEM((2, 64, BLK), F32), pltpu.VMEM((2, 64, BLK), F32),
        ],
        compiler_params=params(1),
        cost_estimate=cost(5 * seq * seq * 128 * 2, seq * 128 * 20, seq * seq),
        name=f"attn_bwd{p}",
    )(q_t, do_t, o_t, lse, k_t, v_t, cos_t, sin_t)


def gw_kernel(dq_ref, dk_ref, dv_ref, r_ref, gw_out, acc_scr):
    i = pl.program_id(0)
    lhs = jnp.concatenate([dq_ref[...], dk_ref[...], dv_ref[...]], axis=0)
    part = dot_nn(lhs, r_ref[...])

    @pl.when(i == 0)
    def _():
        acc_scr[...] = part

    @pl.when(i > 0)
    def _():
        acc_scr[...] += part

    @pl.when(i == pl.num_programs(0) - 1)
    def _():
        gw_out[...] = acc_scr[...].T


def gw_call(dq, dk, dv, r_all):
    seq, hidden = r_all.shape
    spec = pl.BlockSpec((128, BLK), lambda i: (0, i))
    return pl.pallas_call(
        gw_kernel,
        out_shape=jax.ShapeDtypeStruct((hidden, 384), F32),
        grid=(seq // BLK,),
        in_specs=[spec, spec, spec, pl.BlockSpec((BLK, hidden), lambda i: (i, 0))],
        out_specs=pl.BlockSpec((hidden, 384), lambda i: (0, 0)),
        scratch_shapes=[pltpu.VMEM((384, hidden), F32)],
        compiler_params=params(1),
        cost_estimate=cost(2 * seq * hidden * 384, seq * hidden * 2),
        name="gwqkv",
    )(dq, dk, dv, r_all)


def place_kernel(a_ref, b_ref, out):
    out[:, 0:128] = a_ref[0]
    out[:, 128:256] = b_ref[0]


def place_call(gw0, gw1):
    ndev, hidden, _ = gw0.shape
    spec = pl.BlockSpec((1, hidden, 128), lambda w, d: (d, 0, w))
    return pl.pallas_call(
        place_kernel,
        out_shape=jax.ShapeDtypeStruct((hidden, 3 * ndev * 256), F32),
        grid=(3, ndev),
        in_specs=[spec, spec],
        out_specs=pl.BlockSpec((hidden, 256), lambda w, d: (0, w * ndev + d)),
        compiler_params=params(2),
        name="place",
    )(gw0, gw1)


def dx_kernel(a_ref, b_ref, wq_ref, wk_ref, wv_ref, x_ref, inv_ref, g_ref, dy_ref, dx_out, gg_out, acc_scr):
    s = pl.program_id(0)
    a = a_ref[0]
    b = b_ref[0]
    part = None
    for which, w in enumerate((wq_ref, wk_ref, wv_ref)):
        cols = slice(128 * which, 128 * which + 128)
        lhs = jnp.concatenate([a[:, cols], b[:, cols]], axis=1)
        term = dot_nt(lhs, w[...])
        part = term if part is None else part + term

    @pl.when(s == 0)
    def _():
        acc_scr[...] = part

    @pl.when(s > 0)
    def _():
        acc_scr[...] += part

    @pl.when(s == pl.num_programs(0) - 1)
    def _():
        dn = acc_scr[...]
        inv = inv_ref[...]
        x_hat = x_ref[...].astype(F32) * inv
        gg_out[...] = jnp.sum(dn * x_hat, axis=0, keepdims=True)
        d_hat = dn * g_ref[...]
        mean = jnp.mean(d_hat * x_hat, axis=-1, keepdims=True)
        dx_out[...] = (dy_ref[...].astype(F32) + inv * (d_hat - x_hat * mean)).astype(BF16)


def dx_call(d0, d1, w_qkv, x, inv_rms, gain, dy):
    ndev, piece, _ = d0.shape
    hidden = w_qkv.shape[0]
    dspec = pl.BlockSpec((1, piece, 384), lambda s: (s, 0, 0))
    wspec = lambda which: pl.BlockSpec((hidden, 256), lambda s: (0, which * ndev + s))
    whole = lambda *shape: pl.BlockSpec(shape, lambda s: (0, 0))
    return pl.pallas_call(
        dx_kernel,
        out_shape=(jax.ShapeDtypeStruct((piece, hidden), BF16), jax.ShapeDtypeStruct((1, hidden), F32)),
        grid=(ndev,),
        in_specs=[dspec, dspec, wspec(0), wspec(1), wspec(2), whole(piece, hidden), whole(piece, 1), whole(1, hidden), whole(piece, hidden)],
        out_specs=(whole(piece, hidden), whole(1, hidden)),
        scratch_shapes=[pltpu.VMEM((piece, hidden), F32)],
        compiler_params=params(1),
        cost_estimate=cost(2 * piece * hidden * 3 * ndev * 256, 40e6),
        name="dx",
    )(d0, d1, w_qkv, w_qkv, w_qkv, x, inv_rms, gain, dy)


def solution(mesh):
    ndev = mesh.shape['cp']

    def device_fn(x_in, positions, long_factor, norm_gain, w_qkv, w_out, grad_y):
        _, piece, hidden = x_in.shape
        seq = piece * ndev
        dev = lax.axis_index('cp').astype(jnp.int32).reshape(1)
        x = x_in[0]
        dy = grad_y[0]
        x_float = x.astype(F32)
        inv_rms = lax.rsqrt(jnp.mean(x_float * x_float, axis=-1, keepdims=True) + NORM_EPS)
        normed = (x_float * inv_rms * norm_gain).astype(BF16)
        r_all = lax.all_gather(normed, 'cp', axis=0, tiled=True)
        dy_all = lax.all_gather(dy, 'cp', axis=0, tiled=True)

        pos_all = lax.all_gather(positions, 'cp', axis=0, tiled=True)
        half = long_factor.shape[0]
        exponent = jnp.arange(half, dtype=F32) * (1.0 / half)
        inv_freq = 1.0 / (long_factor * jnp.power(10000.0, exponent))
        angles = inv_freq[:, None] * pos_all.astype(F32)[None, :]
        cos_t = jnp.cos(angles) * MSCALE
        sin_t = jnp.sin(angles) * MSCALE

        q_t, k_t, v_t, k_n = qkv_call(dev, r_all, w_qkv, cos_t, sin_t)
        o_t, o_n, lse = fwd_call(q_t, k_n, v_t)
        o_parts = lax.all_to_all(o_n.reshape(ndev, piece, 256), 'cp', 0, 0)
        y_out = y_call(o_parts, w_out, x)
        do_t, gw_own = do_call(dev, dy_all, w_out, o_t)
        g_wout = lax.all_gather(gw_own, 'cp', axis=0, tiled=True)

        gws, dns = [], []
        for p in range(2):
            dq, dk, dv, dn = bwd_call(p, q_t, do_t, o_t, lse, k_t, v_t, cos_t, sin_t)
            dns.append(lax.all_to_all(dn.reshape(ndev, piece, 384), 'cp', 0, 0))
            gws.append(lax.all_gather(gw_call(dq, dk, dv, r_all), 'cp'))
        grad_x, gg = dx_call(dns[0], dns[1], w_qkv, x, inv_rms, norm_gain.reshape(1, hidden), dy)
        g_gain = lax.psum(gg.reshape(hidden), 'cp')
        g_wqkv = place_call(gws[0], gws[1])
        return y_out[None], grad_x[None], g_gain, g_wqkv, g_wout

    seq_spec = P('dp', 'cp', None)
    return jax.shard_map(device_fn, mesh=mesh, in_specs=(seq_spec, P(('dp', 'cp')), P(None), P(None), P(None, None), P(None, None), seq_spec), out_specs=(seq_spec, seq_spec, P('dp'), P('dp', None), P('dp', None)), check_vma=False)
```

time: 5060 us -> 983 us (0.19)
  waiting for transfers between devices: 3990 us -> 151 us
  Pallas kernels: 0 us -> 574 us
  starting transfers between devices: 317 us -> 4.08 us
  matrix products: 293 us -> 0 us
  local copies, waits for them, and re-layouts: 301 us -> 15.2 us
  blocking collectives: 23 us -> 214 us
  other arithmetic: 106 us -> 9.13 us
    ppermute x44 -> x0, waiting for transfers between devices: 3310 us -> none  [the longest x7 2080 us: bwd_step(): k_cur = lax.ppermute(k_cur, 'cp', shift_perm)]
    psum x1 -> x0, waiting for transfers between devices: 680 us -> none  [device_fn(): g_gain, g_wqkv, g_wout = lax.psum((g_gain, g_wqkv, g_wout), 'cp')]
    pallas_call x0 -> x10, Pallas kernels: none -> 574 us  [the longest x2 229 us: bwd_call(): pl.pallas_call(bwd_kernel, out_shape=(tr, tr, tr, jax.ShapeDtypeStruct((s...]
    ppermute x44 -> x0, starting transfers between devices: 317 us -> none  [the longest x7 97 us: fwd_step(): v_cur = lax.ppermute(v_cur, 'cp', shift_perm)]
    dot_general x12 -> x0, matrix products: 293 us -> none  [the longest x1 43.4 us: bwd_block(): jnp.einsum('bqhd,bkhd->bhqk', d_attn, v_blk, preferred_element_type=jnp.f...]
    while x42 -> x0, local copies, waits for them, and re-layouts: 194 us -> none
    all_to_all x0 -> x2, blocking collectives: none -> 178 us  [the longest x1 108 us: device_fn(): dns.append(lax.all_to_all(dn.reshape(ndev, piece, 384), 'cp', 0, 0))]
    all_gather x0 -> x5, waiting for transfers between devices: none -> 104 us  [the longest x1 104 us: device_fn(): r_all = lax.all_gather(normed, 'cp', axis=0, tiled=True)]
  transfers between devices with their start and end apart: 45 -> 6, of which waited for: 31 -> 2; matrix products, arithmetic and copies ran while one was open for 3% -> 0% of each run, Pallas kernels for 0% -> 52%
where the time goes in v1:
time: 983 us; the launch traced here: 981 us
  Pallas kernels  574 us (58%)
  blocking collectives  214 us (22%)
  waiting for transfers between devices  151 us (15%)
  local copies, waits for them, and re-layouts  15.2 us (2%)
  between operations  13.9 us (1%)
    pallas_call x2, Pallas kernels, bwd_call(): pl.pallas_call(bwd_kernel, out_shape=(tr, tr, tr, jax.ShapeDtypeStruct((s...  229 us
    pallas_call x1, Pallas kernels, fwd_call(): pl.pallas_call(fwd_kernel, out_shape=(jax.ShapeDtypeStruct((width, seq),...  156 us
    all_to_all x1, blocking collectives, device_fn(): dns.append(lax.all_to_all(dn.reshape(ndev, piece, 384), 'cp', 0, 0))  108 us
    all_gather x1, waiting for transfers between devices, device_fn(): r_all = lax.all_gather(normed, 'cp', axis=0, tiled=True)  104 us
    all_to_all x1, blocking collectives, device_fn(): o_parts = lax.all_to_all(o_n.reshape(ndev, piece, 256), 'cp', 0, 0)  70.1 us
    all_to_all x1, waiting for transfers between devices, device_fn(): dns.append(lax.all_to_all(dn.reshape(ndev, piece, 384), 'cp', 0, 0))  46.3 us
    pallas_call x2, Pallas kernels, gw_call(): pl.pallas_call(gw_kernel, out_shape=jax.ShapeDtypeStruct((hidden, 384), F...  44.7 us
    pallas_call x1, Pallas kernels, place_call(): pl.pallas_call(place_kernel, out_shape=jax.ShapeDtypeStruct((hidden, 3 *...  40.8 us
  transfers between devices with their start and end apart: 6, of which 2 were waited for; matrix products, arithmetic and copies ran while one was open for 0% of the time, Pallas kernels for 52%

profile of v1, /device:TPU:0, one launch (start us, length us, event | category | flops | bytes accessed | tf_op | source)
XLA Modules:
  0.0 981.1 jit_solution(5296953445664520903)
XLA Ops:
  7.2 0.0 copy-start
  7.2 0.0 copy-start.4
  7.2 0.0 all-gather.10.cloned.1.call-start
  7.2 2.7 fusion
  10.0 0.0 copy-start.2
  10.0 0.6 copy-done.2
  10.6 0.0 copy-done
  10.6 0.0 copy-done.4
  10.6 2.4 fusion.2
  13.0 0.0 copy-start.5
  13.0 0.0 copy-start.6
  13.0 0.0 all-gather.10.cloned.1.call-update
  13.0 0.0 all-gather.14.cloned.1.call-start
  13.1 0.7 all-gather.14.cloned.1.call-update
  13.8 0.0 all-gather.12.cloned.1.call-start
  13.8 0.0 copy-done.5
  13.9 13.7 %all-gather.3 = s32[8,1,768]{2,1,0:T(1,128)S(1)} all-gather(s32[1,1,768]{2,1,0:T(1,128)S(1)} %reshape.58), channel_id=1, replica_groups=mesh['dp'=1,'cp'=8] {'cp'}, dimensions={0}, use_global_device_ids=true | all-gather | bytes 27648 | tf_op jit(solution)/shard_map/all_gather | solution.py:461
  27.6 0.0 copy-done.6
  27.6 3.9 fusion.4
  31.5 104.2 %all-gather.10.cloned.1.call-done.r_ref = bf16[6144,2048]{1,0:T(8,128)(2,1)} async-done(((bf16[768,2048]{1,0:T(8,128)(2,1)}), bf16[6144,2048]{1,0:T(8,128)(2,1)}) %all-gather.10.cloned.1.call-update) | async-done | bytes 25165840 | tf_op jit(solution)/shard_map/all_gather | solution.py:458
  135.7 27.3 %qkv.1 = (bf16[256,6144]{1,0:T(8,128)(2,1)}, bf16[256,6144]{1,0:T(8,128)(2,1)}, bf16[256,6144]{1,0:T(8,128)(2,1)}, bf16[6144,256]{1,0:T(8,128)(2,1)}) custom-call(s32[1]{0:T(128)} %bitcast.d_ref, bf16[6144,2048]{1,0:T(8,128)(2,1)} %all-gather.10.cloned.1.call-done.r_ref, bf16[2048,6144]{1,0:T(8,128)(2,1)} %wv_ref.3, bf16[2048,6144]{1,0:T(8,128)(2,1)} %wv_ref.3, ...), custom_call_target="tpu_custom_call" | custom-call | flops 19327352832 | bytes 37748736 | tf_op jit(solution)/shard_map/qkv/pallas_call | solution.py:72
  163.1 156.3 %attn_fwd.1 = (bf16[256,6144]{1,0:T(8,128)(2,1)}, bf16[6144,256]{1,0:T(8,128)(2,1)}, f32[16,6144]{1,0:T(8,128)}) custom-call(bf16[256,6144]{1,0:T(8,128)(2,1)} %get-tuple-element.24.q_ref, bf16[6144,256]{1,0:T(8,128)(2,1)} %get-tuple-element.25.k_ref, bf16[256,6144]{1,0:T(8,128)(2,1)} %get-tuple-element.26.v_ref), custom_call_target="tpu_custom_call" | custom-call | flops 77309411328 | bytes 15728640 | tf_op jit(solution)/shard_map/attn_fwd/pallas_call | solution.py:142
  319.3 0.0 all-gather.14.cloned.1.call-done
  319.3 22.5 %do_gwout.1 = (bf16[256,6144]{1,0:T(8,128)(2,1)}, f32[256,2048]{1,0:T(8,128)}) custom-call(s32[1]{0:T(128)} %bitcast.d_ref, bf16[6144,2048]{1,0:T(8,128)(2,1)} %bitcast.27, bf16[2048,2048]{1,0:T(8,128)(2,1)} %w_ref.3, bf16[256,6144]{1,0:T(8,128)(2,1)} %get-tuple-element.28.o_ref), custom_call_target="tpu_custom_call" | custom-call | flops 12884901888 | bytes 25165824 | tf_op jit(solution)/shard_map/do_gwout/pallas_call | solution.py:217
  341.8 0.0 all-gather.12.cloned.1.call-update
  341.9 0.2 all-gather.16.cloned.1.call-start
  342.1 114.6 %attn_bwd0.1 = (bf16[128,6144]{1,0:T(8,128)(2,1)}, bf16[128,6144]{1,0:T(8,128)(2,1)}, bf16[128,6144]{1,0:T(8,128)(2,1)}, bf16[6144,384]{1,0:T(8,128)(2,1)}) custom-call(bf16[256,6144]{1,0:T(8,128)(2,1)} %get-tuple-element.24.q_ref, bf16[256,6144]{1,0:T(8,128)(2,1)} %get-tuple-element.29.do_ref, bf16[256,6144]{1,0:T(8,128)(2,1)} %get-tuple-element.28.o_ref, ...), custom_call_target="tpu_custom_call" | custom-call | flops 48318382080 | bytes 15728640 | tf_op jit(solution)/shard_map/attn_bwd0/pallas_call | solution.py:327
  456.7 22.4 %gwqkv.2 = f32[2048,384]{1,0:T(8,128)} custom-call(bf16[128,6144]{1,0:T(8,128)(2,1)} %get-tuple-element.36.dq_ref, bf16[128,6144]{1,0:T(8,128)(2,1)} %get-tuple-element.37.dk_ref, bf16[128,6144]{1,0:T(8,128)(2,1)} %get-tuple-element.38.dv_ref, bf16[6144,2048]{1,0:T(8,128)(2,1)} %all-gather.10.cloned.1.call-done.r_ref), custom_call_target="tpu_custom_call" | custom-call | flops 9663676416 | bytes 25165824 | tf_op jit(solution)/shard_map/gwqkv/pallas_call | solution.py:365
  479.0 0.0 all-gather.16.cloned.1.call-update
  479.0 0.0 all-gather.18.cloned.1.call-start
  479.1 114.4 %attn_bwd1.1 = (bf16[128,6144]{1,0:T(8,128)(2,1)}, bf16[128,6144]{1,0:T(8,128)(2,1)}, bf16[128,6144]{1,0:T(8,128)(2,1)}, bf16[6144,384]{1,0:T(8,128)(2,1)}) custom-call(bf16[256,6144]{1,0:T(8,128)(2,1)} %get-tuple-element.24.q_ref, bf16[256,6144]{1,0:T(8,128)(2,1)} %get-tuple-element.29.do_ref, bf16[256,6144]{1,0:T(8,128)(2,1)} %get-tuple-element.28.o_ref, ...), custom_call_target="tpu_custom_call" | custom-call | flops 48318382080 | bytes 15728640 | tf_op jit(solution)/shard_map/attn_bwd1/pallas_call | solution.py:327
  593.5 22.4 %gwqkv.3 = f32[2048,384]{1,0:T(8,128)} custom-call(bf16[128,6144]{1,0:T(8,128)(2,1)} %get-tuple-element.39.dq_ref, bf16[128,6144]{1,0:T(8,128)(2,1)} %get-tuple-element.40.dk_ref, bf16[128,6144]{1,0:T(8,128)(2,1)} %get-tuple-element.41.dv_ref, bf16[6144,2048]{1,0:T(8,128)(2,1)} %all-gather.10.cloned.1.call-done.r_ref), custom_call_target="tpu_custom_call" | custom-call | flops 9663676416 | bytes 25165824 | tf_op jit(solution)/shard_map/gwqkv/pallas_call | solution.py:365
  615.9 0.0 copy-start.1
  615.9 0.0 all-gather.18.cloned.1.call-update
  615.9 1.9 copy-done.1
  617.8 70.1 %all_to_all.15.o_ref = bf16[8,768,256]{2,1,0:T(8,128)(2,1)} all-to-all(bf16[8,768,256]{2,1,0:T(8,128)(2,1)S(1)} %bitcast.23), channel_id=1, replica_groups=mesh['dp'=1,'cp'=8] {'cp'}, dimensions={0} | all-to-all | bytes 6291456 | tf_op jit(solution)/shard_map/all_to_all | solution.py:471
  687.9 107.6 %all_to_all.16.a_ref = bf16[8,768,384]{2,1,0:T(8,128)(2,1)} all-to-all(bf16[8,768,384]{2,1,0:T(8,128)(2,1)} %bitcast.21), channel_id=1, replica_groups=mesh['dp'=1,'cp'=8] {'cp'}, dimensions={0} | all-to-all | bytes 9437184 | tf_op jit(solution)/shard_map/all_to_all | solution.py:479
  795.5 0.0 copy-start.3
  795.5 3.7 all-to-all-start.2
  799.3 0.0 copy-done.3
  799.3 0.9 rsqrt.7.inv_ref
  800.2 17.2 %y_proj.1 = bf16[768,2048]{1,0:T(8,128)(2,1)} custom-call(bf16[8,768,256]{2,1,0:T(8,128)(2,1)} %all_to_all.15.o_ref, bf16[2048,2048]{1,0:T(8,128)(2,1)} %w_ref.3, bf16[768,2048]{1,0:T(8,128)(2,1)} %bitcast.16), custom_call_target="tpu_custom_call" | custom-call | flops 6442450944 | bytes 20000000 | tf_op jit(solution)/shard_map/y_proj/pallas_call | solution.py:183
  817.4 46.3 %all-to-all-done.2.b_ref = bf16[8,768,384]{2,1,0:T(8,128)(2,1)} async-done(((bf16[8,768,384]{2,1,0:T(8,128)(2,1)}), bf16[8,768,384]{2,1,0:T(8,128)(2,1)}, u32[]{:S(2)}, u32[]{:S(2)}) %all-to-all-start.2) | async-done | bytes 4718624 | tf_op jit(solution)/shard_map/all_to_all | solution.py:479
  863.7 35.8 %dx.1 = (bf16[768,2048]{1,0:T(8,128)(2,1)}, f32[1,2048]{1,0:T(1,128)}) custom-call(bf16[8,768,384]{2,1,0:T(8,128)(2,1)} %all_to_all.16.a_ref, bf16[8,768,384]{2,1,0:T(8,128)(2,1)} %all-to-all-done.2.b_ref, bf16[2048,6144]{1,0:T(8,128)(2,1)} %wv_ref.3, bf16[2048,6144]{1,0:T(8,128)(2,1)} %wv_ref.3, bf16[2048,6144]{1,0:T(8,128)(2,1)} %wv_ref.3, ...), custom_call_target="tpu_custom_call" | custom-call | flops 19327352832 | bytes 40000000 | tf_op jit(solution)/shard_map/dx/pallas_call | solution.py:433
  899.6 22.5 %psum.7 = f32[2048]{0:T(1024)} all-reduce(f32[2048]{0:T(1024)} %bitcast.26), channel_id=1, replica_groups=mesh['dp'=1,'cp'=8] {'cp'}, use_global_device_ids=true, to_apply=%region_1.0 | all-reduce | flops 2048 | bytes 16384 | tf_op jit(solution)/shard_map/psum | solution.py:482
  922.0 0.0 all-gather.18.cloned.1.call-done
  922.1 40.8 %place.1 = f32[2048,6144]{1,0:T(8,128)} custom-call(f32[8,2048,384]{2,1,0:T(8,128)} %bitcast.18, f32[8,2048,384]{2,1,0:T(8,128)} %bitcast.19), custom_call_target="tpu_custom_call" | custom-call | tf_op jit(solution)/shard_map/place/pallas_call | solution.py:386
  962.8 11.8 %copy.15 = f32[2048,2048]{1,0:T(8,128)} copy(f32[2048,2048]{1,0:T(8,128)} %all-gather.12.cloned.1.call-done) | data formatting | bytes 33554432
  (6 shorter events, 0.0 us)
Async XLA Ops:
  7.2 3.4 copy-start
  7.2 3.4 copy-start.4
  7.2 128.5 %all-gather.10.cloned.1.call-start = ((), (), s32[]{:S(2)}) async-start(), calls=%async_computation.3 | async-start | bytes 28311552 | tf_op jit(solution)/shard_map/all_gather | solution.py:458
  10.0 0.6 copy-start.2
  13.0 0.8 copy-start.5
  13.0 14.5 %copy-start.6 = (f32[32]{0:T(128)S(1)}, f32[32]{0:T(128)}, u32[]{:S(2)}) copy-start(f32[32]{0:T(128)} %param.9) | copy-start | bytes 388
  13.0 306.3 %all-gather.14.cloned.1.call-start = ((), (), s32[]{:S(2)}) async-start(), calls=%async_computation.5 | async-start | bytes 28311552 | tf_op jit(solution)/shard_map/all_gather | solution.py:459
  13.8 908.2 %all-gather.12.cloned.1.call-start = ((), (), s32[]{:S(2)}) async-start(), calls=%async_computation.4 | async-start | bytes 18874368 | tf_op jit(solution)/shard_map/all_gather | solution.py:474
  341.9 580.2 %all-gather.16.cloned.1.call-start = ((), (), s32[]{:S(2)}) async-start(), calls=%async_computation.6 | async-start | bytes 28311552 | tf_op jit(solution)/shard_map/all_gather | solution.py:480
  479.0 443.0 %all-gather.18.cloned.1.call-start = ((), (), s32[]{:S(2)}) async-start(), calls=%async_computation.7 | async-start | bytes 28311552 | tf_op jit(solution)/shard_map/all_gather | solution.py:480
  615.9 1.9 copy-start.1
  795.5 3.7 copy-start.3
  795.5 68.2 %all-to-all-start.2 = ((bf16[8,768,384]{2,1,0:T(8,128)(2,1)}), bf16[8,768,384]{2,1,0:T(8,128)(2,1)}, u32[]{:S(2)}, u32[]{:S(2)}) async-start(bf16[8,768,384]{2,1,0:T(8,128)(2,1)} %bitcast.22), calls=%async_computation.2 | async-start | bytes 9437184 | tf_op jit(solution)/shard_map/all_to_all | solution.py:479
Sparse Core Ops, SparseCore 0:
  13.2 122.5 all-gather.9
  137.5 119.7 all-gather.13
  342.0 84.0 all-gather.11
  479.2 119.6 all-gather.15
  616.1 208.9 all-gather.17

commit v2 on v0

v2 whole, which is shorter than its diff:
```python
import math
import jax
import jax.numpy as jnp
from jax import lax
from jax.experimental import pallas as pl
from jax.experimental.pallas import tpu as pltpu
from jax.sharding import PartitionSpec as P

NORM_EPS = 1e-5
MSCALE = math.sqrt(1.0 + math.log(32.0) / math.log(4096.0))
MASK_VALUE = -1e30
LOG2E = math.log2(math.e)
BF16 = jnp.bfloat16
F32 = jnp.float32
BLK = 512
VMEM_LIMIT = 60 * 1024 * 1024


def dot_nn(a, b):
    return lax.dot_general(a, b, (((1,), (0,)), ((), ())), preferred_element_type=F32)


def dot_nt(a, b):
    return lax.dot_general(a, b, (((1,), (1,)), ((), ())), preferred_element_type=F32)


def params(n=1, **kw):
    return pltpu.CompilerParams(dimension_semantics=("arbitrary",) * n, vmem_limit_bytes=VMEM_LIMIT, **kw)


def cost(flops, nbytes, trans=0):
    return pl.CostEstimate(flops=int(flops), bytes_accessed=int(nbytes), transcendentals=int(trans))


MESH = pl.DeviceIdType.MESH


class Grid:
    def __init__(self):
        self.me = lax.axis_index('cp')
        self.core = self.me % 2
        self.x = (self.me // 2) % 2
        self.y = self.me // 4

    def flip(self, yf, xf, cf):
        return ((self.y + yf) % 2) * 4 + ((self.x + xf) % 2) * 2 + (self.core + cf) % 2

    def xor(self, mask):
        return self.flip(mask // 4, (mask // 2) % 2, mask % 2)


def barrier(grid, masks):
    sem = pltpu.get_barrier_semaphore()
    for mask in masks:
        pl.semaphore_signal(sem, inc=1, device_id={'cp': grid.xor(mask)}, device_id_type=MESH)
    pl.semaphore_wait(sem, len(masks))


class Gather:
    SENDS = {
        'xA': (0, 0, 1, 2), 'yB': (0, 1, 1, 4), 'xB': (0, 1, 1, 2), 'yA': (0, 0, 1, 4), 'own': (0, 0, 2, 1),
        'dA': (2, 0, 1, 4), 'dB': (4, 1, 1, 2),
        'cxA': (2, 0, 1, 1), 'cyB': (4, 1, 1, 1), 'cxB': (2, 1, 1, 1), 'cyA': (4, 0, 1, 1), 'cdA': (6, 0, 1, 1), 'cdB': (6, 1, 1, 1),
    }
    ORDER = tuple(SENDS)

    def __init__(self, grid, src, dst, ssem, rsem):
        self.grid, self.src, self.dst, self.ssem, self.rsem = grid, src, dst, ssem, rsem

    def desc(self, name, arriving=False):
        mask, first, halves, target = self.SENDS[name]
        k = self.ORDER.index(name)
        dst = self.dst(self.grid.xor(mask ^ target if arriving else mask), first, halves)
        src = dst if (mask or arriving or self.src is None) else self.src(first, halves)
        return pltpu.make_async_remote_copy(src, dst, self.ssem(k), self.rsem(k), device_id={'cp': self.grid.xor(target)}, device_id_type=MESH)

    def send(self, *names):
        for name in names:
            self.desc(name).start()

    def arrived(self, *names):
        for name in names:
            self.desc(name, True).wait_recv()

    def begin(self):
        self.send('xA', 'yB', 'xB', 'yA', 'own')

    def first(self):
        self.arrived('xA', 'yB')
        self.send('dA', 'dB', 'cxA', 'cyB')

    def second(self):
        self.arrived('xB', 'yA')
        self.send('cxB', 'cyA')

    def third(self):
        self.arrived('dA', 'dB')
        self.send('cdA', 'cdB')

    def last(self):
        self.arrived('own', 'cxA', 'cyB', 'cxB', 'cyA', 'cdA', 'cdB')
        self.sent()

    def sent(self):
        for name in self.ORDER:
            self.desc(name).wait_send()


def row_gather(grid, src, dst, piece, ssem, rsem):
    half = piece // 2

    def place(owner, first, halves):
        return dst.at[pl.ds(pl.multiple_of(owner * piece + first * half, half), halves * half)]

    own = None if src is None else lambda first, halves: src.at[pl.ds(first * half, halves * half)]
    return Gather(grid, own, place, lambda k: ssem.at[k], lambda k: rsem.at[k])


GATHER_SEMS = [pltpu.SemaphoreType.DMA((13,)), pltpu.SemaphoreType.DMA((13,))]


def qkv_kernel(r_own, pos_ref, inv_ref, w_hbm, r_all, q_hbm, k_hbm, v_hbm, kn_hbm, cos_hbm, sin_hbm,
               wtmp, w_scr, rbuf, pos_scr, q_st, k_st, v_st, kn_st, cos_st, sin_st, wsem, lsem, osem, csem, pssem, prsem, ssem, rsem):
    grid = Grid()
    piece, hidden = r_own.shape
    hp = piece // 2
    width = wtmp.shape[2]
    ndev = r_all.shape[0] // piece

    def w_copy(which):
        cols = pl.ds(pl.multiple_of(which * ndev * width + grid.me * width, width), width)
        return pltpu.make_async_copy(w_hbm.at[:, cols], wtmp.at[which], wsem.at[which])

    for which in range(3):
        w_copy(which).start()
    barrier(grid, range(1, 8))
    gather = row_gather(grid, r_own, r_all, piece, ssem, rsem)
    gather.begin()

    def pos_copy(mask, owner):
        return pltpu.make_async_remote_copy(pos_ref, pos_scr.at[pl.ds(2 * owner, 2)], pssem.at[mask], prsem.at[mask], device_id={'cp': grid.xor(mask)}, device_id_type=MESH)

    for mask in range(1, 8):
        pos_copy(mask, grid.me).start()
    pos_scr[pl.ds(2 * grid.me, 2)] = pos_ref[...]
    for which in range(3):
        w_copy(which).wait()
        w_scr[width * which:width * (which + 1)] = wtmp[which].T
    for mask in range(1, 8):
        pos_copy(mask, grid.xor(mask)).wait_recv()

    inv = inv_ref[...]
    nh = width // 64

    def group(g, carry):
        stage = g // 2
        one = (stage + 2) // 3
        two = stage // 3
        flips = ((two, one), (one, two))
        half0 = (stage // 2) * (1 - two)
        halves = (half0, 1 - half0)
        owners = [grid.flip(yf, xf, g % 2) for yf, xf in flips]
        offs = [pl.multiple_of(owners[u] * piece + halves[u] * hp, 128) for u in range(2)]

        def load(u):
            return pltpu.make_async_copy(r_all.at[pl.ds(offs[u], hp)], rbuf.at[u], lsem.at[u])

        def keep(u):
            return pltpu.make_async_copy(rbuf.at[u], r_all.at[pl.ds(offs[u], hp)], csem.at[u])

        @pl.when(g == 0)
        def _():
            for u in range(2):
                pltpu.make_async_copy(r_own.at[pl.ds(u * hp, hp)], rbuf.at[u], lsem.at[u]).start()

        @pl.when(g == 1)
        def _():
            gather.arrived('own')

        @pl.when(g == 2)
        def _():
            gather.first()

        @pl.when(g == 3)
        def _():
            gather.arrived('cxA', 'cyB')

        @pl.when(g == 4)
        def _():
            gather.second()

        @pl.when(g == 5)
        def _():
            gather.arrived('cxB', 'cyA')

        @pl.when(g == 6)
        def _():
            gather.third()

        @pl.when(g == 7)
        def _():
            gather.arrived('cdA', 'cdB')

        @pl.when(g > 0)
        def _():
            for u in range(2):
                load(u).start()

        outs = []
        for u in range(2):
            load(u).wait()

            @pl.when(g == 0)
            def _():
                keep(u).start()

            angles = inv * pos_scr[2 * owners[u] + halves[u]].astype(F32)
            cos = jnp.cos(angles) * MSCALE
            sin = jnp.sin(angles) * MSCALE
            cos_st[u] = cos
            sin_st[u] = sin
            r_blk = rbuf[u]

            def rope(t):
                rows = []
                for h in range(nh):
                    t1 = t[64 * h:64 * h + 32]
                    t2 = t[64 * h + 32:64 * h + 64]
                    rows += [t1 * cos - t2 * sin, t2 * cos + t1 * sin]
                return jnp.concatenate(rows, axis=0).astype(BF16)

            q_st[u] = rope(dot_nt(w_scr[0:width], r_blk)) * BF16(0.125)
            k_rot = rope(dot_nt(w_scr[width:2 * width], r_blk))
            k_st[u] = k_rot
            kn_st[u] = k_rot.T
            v_st[u] = dot_nt(w_scr[2 * width:], r_blk).astype(BF16)
            for n, (st, hbm) in enumerate(((q_st, q_hbm), (k_st, k_hbm), (v_st, v_hbm), (cos_st, cos_hbm), (sin_st, sin_hbm))):
                outs.append(pltpu.make_async_copy(st.at[u], hbm.at[:, pl.ds(offs[u], hp)], osem.at[u, n]))
            outs.append(pltpu.make_async_copy(kn_st.at[u], kn_hbm.at[pl.ds(offs[u], hp)], osem.at[u, 5]))
            for copy in outs[6 * u:]:
                copy.start()
        for copy in outs:
            copy.wait()

        @pl.when(g == 0)
        def _():
            for u in range(2):
                keep(u).wait()

        return carry

    lax.fori_loop(0, 8, group, 0)
    gather.sent()
    for mask in range(1, 8):
        pos_copy(mask, grid.me).wait_send()


def qkv_call(r_own, pos, inv_freq, w_qkv):
    piece, hidden = r_own.shape
    ndev = 8
    seq = piece * ndev
    hp = piece // 2
    width = 256
    half = inv_freq.shape[0]
    tr = jax.ShapeDtypeStruct((width, seq), BF16)
    tab = jax.ShapeDtypeStruct((half, seq), F32)
    hbm = pl.BlockSpec(memory_space=pl.ANY)
    vmem = pl.BlockSpec(memory_space=pltpu.VMEM)
    dma = pltpu.SemaphoreType.DMA
    return pl.pallas_call(
        qkv_kernel,
        out_shape=(jax.ShapeDtypeStruct((seq, hidden), BF16), tr, tr, tr, jax.ShapeDtypeStruct((seq, width), BF16), tab, tab),
        in_specs=[hbm, vmem, vmem, hbm],
        out_specs=(hbm,) * 7,
        scratch_shapes=[
            pltpu.VMEM((3, hidden, width), BF16), pltpu.VMEM((3 * width, hidden), BF16), pltpu.VMEM((2, hp, hidden), BF16),
            pltpu.VMEM((2 * ndev, 1, hp), jnp.int32),
            pltpu.VMEM((2, width, hp), BF16), pltpu.VMEM((2, width, hp), BF16), pltpu.VMEM((2, width, hp), BF16), pltpu.VMEM((2, hp, width), BF16),
            pltpu.VMEM((2, half, hp), F32), pltpu.VMEM((2, half, hp), F32),
            dma((3,)), dma((2,)), dma((2, 6)), dma((2,)), dma((8,)), dma((8,)),
        ] + GATHER_SEMS,
        compiler_params=pltpu.CompilerParams(collective_id=0, has_side_effects=True, vmem_limit_bytes=VMEM_LIMIT),
        cost_estimate=cost(2 * seq * hidden * 3 * width, 2 * seq * hidden * 2 + seq * width * 8),
        name="gather_qkv",
    )(r_own, pos.reshape(2, 1, hp), inv_freq.reshape(half, 1), w_qkv)


FWD_FIRST, FWD_SECOND, FWD_THIRD = 8, 11, 20


def fwd_kernel(q_ref, k_ref, v_ref, dy_own, o_out, on_out, lse_out, dy_all, qz_scr, acc_scr, m_scr, l_scr, keep, ksem, ssem, rsem):
    i = pl.program_id(1)
    t = pl.program_id(0) * pl.num_programs(1) + i
    grid = Grid()
    gather = row_gather(grid, dy_own, dy_all, dy_own.shape[0], ssem, rsem)
    keep_in = pltpu.make_async_copy(dy_own, keep, ksem)
    keep_out = pltpu.make_async_copy(keep, gather.dst(grid.me, 0, 2), ksem)

    @pl.when(t == 0)
    def _():
        barrier(grid, (1, 2, 4))
        gather.begin()
        keep_in.start()

    @pl.when(t == 1)
    def _():
        keep_in.wait()
        keep_out.start()

    @pl.when(t == FWD_FIRST)
    def _():
        gather.first()
        keep_out.wait()

    @pl.when(t == FWD_SECOND)
    def _():
        gather.second()

    @pl.when(t == FWD_THIRD)
    def _():
        gather.third()

    @pl.when(t == pl.num_programs(0) * pl.num_programs(1) - 1)
    def _():
        gather.last()

    q_blk = q_ref[...]
    zero = jnp.zeros((64, BLK), BF16)
    qz_scr[0] = jnp.concatenate([q_blk[0:64], zero], axis=0)
    qz_scr[1] = jnp.concatenate([zero, q_blk[64:128]], axis=0)
    acc_scr[...] = jnp.zeros_like(acc_scr)
    m_scr[...] = jnp.full_like(m_scr, MASK_VALUE)
    l_scr[...] = jnp.zeros_like(l_scr)

    def step(j, masked):
        off = pl.multiple_of(j * BLK, BLK)
        k_blk = k_ref[pl.ds(off, BLK), :]
        scores = [dot_nn(k_blk, qz_scr[h]) * LOG2E for h in range(2)]
        for h in range(2):
            s = scores[h]
            if masked:
                krow = lax.broadcasted_iota(jnp.int32, s.shape, 0)
                qcol = lax.broadcasted_iota(jnp.int32, s.shape, 1)
                s = jnp.where(krow <= qcol, s, MASK_VALUE)
            m_old = m_scr[h:h + 1, :]
            m_new = jnp.maximum(m_old, jnp.max(s, axis=0, keepdims=True))
            m_scr[h:h + 1, :] = m_new
            alpha = jnp.exp2(m_old - m_new)
            p = jnp.exp2(s - m_new)
            l_scr[h:h + 1, :] = l_scr[h:h + 1, :] * alpha + jnp.sum(p, axis=0, keepdims=True)
            pv = dot_nn(v_ref[64 * h:64 * h + 64, pl.ds(off, BLK)], p.astype(BF16))
            acc_scr[h] = acc_scr[h] * alpha + pv

    def body(j, carry):
        step(j, False)
        return carry

    lax.fori_loop(0, i, body, 0)
    step(i, True)
    outs = []
    for h in range(2):
        l = l_scr[h:h + 1, :]
        outs.append((acc_scr[h] / l).astype(BF16))
        lse_out[h:h + 1, :] = m_scr[h:h + 1, :] * (1.0 / LOG2E) + jnp.log(l)
    o_blk = jnp.concatenate(outs, axis=0)
    o_out[...] = o_blk
    on_out[...] = o_blk.T


def fwd_call(q_t, k_n, v_t, dy):
    width, seq = q_t.shape
    piece, hidden = dy.shape
    pairs = width // 128
    nblk = seq // BLK
    return pl.pallas_call(
        fwd_kernel,
        out_shape=(jax.ShapeDtypeStruct((width, seq), BF16), jax.ShapeDtypeStruct((seq, width), BF16), jax.ShapeDtypeStruct((8 * pairs, seq), F32), jax.ShapeDtypeStruct((seq, hidden), BF16)),
        grid=(pairs, nblk),
        in_specs=[
            pl.BlockSpec((128, BLK), lambda p, i: (p, i)),
            pl.BlockSpec((seq, 128), lambda p, i: (0, p)),
            pl.BlockSpec((128, seq), lambda p, i: (p, 0)),
            pl.BlockSpec(memory_space=pl.ANY),
        ],
        out_specs=(
            pl.BlockSpec((128, BLK), lambda p, i: (p, i)),
            pl.BlockSpec((BLK, 128), lambda p, i: (i, p)),
            pl.BlockSpec((8, BLK), lambda p, i: (p, i)),
            pl.BlockSpec(memory_space=pl.ANY),
        ),
        scratch_shapes=[
            pltpu.VMEM((2, 128, BLK), BF16), pltpu.VMEM((2, 64, BLK), F32), pltpu.VMEM((8, BLK), F32), pltpu.VMEM((8, BLK), F32),
            pltpu.VMEM((piece, hidden), BF16), pltpu.SemaphoreType.DMA,
        ] + GATHER_SEMS,
        compiler_params=params(2, collective_id=1, has_side_effects=True),
        cost_estimate=cost(2 * 2 * seq * seq * width * 2, seq * width * 10, seq * seq),
        name="attn_fwd",
    )(q_t, k_n, v_t, dy)


def y_kernel(d_ref, o_ref, own_ref, w_ref, x_ref, y_out, acc_scr):
    s = pl.program_id(0)
    part = dot_nn(jnp.where(s == d_ref[0], own_ref[...], o_ref[0]), w_ref[...])

    @pl.when(s == 0)
    def _():
        acc_scr[...] = part

    @pl.when(s > 0)
    def _():
        acc_scr[...] += part

    @pl.when(s == pl.num_programs(0) - 1)
    def _():
        y_out[...] = (x_ref[...].astype(F32) + acc_scr[...]).astype(BF16)


def y_call(dev, o_parts, o_n, w_out, x):
    ndev, piece, width = o_parts.shape
    hidden = w_out.shape[1]
    return pl.pallas_call(
        y_kernel,
        out_shape=jax.ShapeDtypeStruct((piece, hidden), BF16),
        grid_spec=pltpu.PrefetchScalarGridSpec(
            num_scalar_prefetch=1,
            grid=(ndev,),
            in_specs=[
                pl.BlockSpec((1, piece, width), lambda s, d: (s, 0, 0)),
                pl.BlockSpec((piece, width), lambda s, d: (d[0], 0)),
                pl.BlockSpec((width, hidden), lambda s, d: (s, 0)),
                pl.BlockSpec((piece, hidden), lambda s, d: (0, 0)),
            ],
            out_specs=pl.BlockSpec((piece, hidden), lambda s, d: (0, 0)),
            scratch_shapes=[pltpu.VMEM((piece, hidden), F32)],
        ),
        compiler_params=params(1),
        cost_estimate=cost(2 * piece * hidden * ndev * width, 20e6),
        name="y_proj",
    )(dev, o_parts, o_n, w_out, x)


def split3(value):
    hi = value.astype(BF16).astype(F32)
    mid = (value - hi).astype(BF16).astype(F32)
    return hi, mid, value - hi - mid


HEADS = 4
HD = 64
FIRST, SECOND, THIRD = 6, 9, 2


def bwd_kernel(dy_ref, r_ref, q_ref, o_ref, k_ref, v_ref, lse_ref, cos_ref, sin_ref, w_hbm, on_hbm,
               o_recv, gwo_all, dn_recv, gw_all,
               do_scr, w_scr, gwo_scr, qa_scr, doa_scr, ka_scr, va_scr, dq_scr, dk_scr, dv_scr, dn_scr, gw_scr,
               wsem, lsem, o_ssem, o_rsem, d_ssem, d_rsem, g_ssem, g_rsem):
    s = pl.program_id(0)
    nblk = do_scr.shape[1] // BLK
    grid = Grid()
    width, hidden = w_scr.shape
    piece = on_hbm.shape[0] // 8
    masks = range(1, 8)
    row64 = lax.broadcasted_iota(jnp.int32, (HD, BLK), 0)

    def blk(t):
        return pl.ds(pl.multiple_of(t * BLK, BLK), BLK)

    def o_copy(mask, owner):
        src = on_hbm.at[pl.ds(pl.multiple_of(grid.xor(mask) * piece, piece), piece)]
        return pltpu.make_async_remote_copy(src, o_recv.at[owner], o_ssem.at[mask], o_rsem.at[mask], device_id={'cp': grid.xor(mask)}, device_id_type=MESH)

    def dn_cols(owner):
        return pl.ds(pl.multiple_of(owner * piece, 128), piece)

    def dn_copy(h, mask, owner):
        src = dn_scr.at[h % 2, :, dn_cols(grid.xor(mask))]
        return pltpu.make_async_remote_copy(src, dn_recv.at[h, owner], d_ssem.at[h, mask], d_rsem.at[h, mask], device_id={'cp': grid.xor(mask)}, device_id_type=MESH)

    def dn_own(h):
        return pltpu.make_async_copy(dn_scr.at[h % 2, :, dn_cols(grid.me)], dn_recv.at[h, grid.me], lsem.at[0])

    def gw_own(h):
        return pltpu.make_async_copy(gw_scr.at[h % 2], gw_all.at[grid.me, h], lsem.at[1])

    def gw_gather(h):
        half = 3 * HD // 2
        return Gather(grid, None, lambda owner, first, halves: gw_all.at[owner, h, pl.ds(first * half, halves * half)], lambda k: g_ssem.at[h, k], lambda k: g_rsem.at[h, k])

    gwo_gather = row_gather(grid, None, gwo_all, width, g_ssem.at[HEADS], g_rsem.at[HEADS])

    @pl.when(s == 0)
    def _():
        w_copy = pltpu.make_async_copy(w_hbm.at[pl.ds(pl.multiple_of(grid.me * width, width), width)], w_scr, wsem)
        w_copy.start()
        barrier(grid, masks)
        for mask in masks:
            o_copy(mask, grid.me).start()
        w_copy.wait()
        gwo_scr[...] = jnp.zeros_like(gwo_scr)

    @pl.when(s < nblk)
    def _():
        cols = blk(s)
        dy = dy_ref[...]
        do_scr[:, cols] = dot_nt(w_scr[...], dy).astype(BF16)
        gwo_scr[...] += dot_nn(o_ref[:, cols], dy)

    @pl.when(s == nblk)
    def _():
        own = pltpu.make_async_copy(gwo_scr, gwo_gather.dst(grid.me, 0, 2), lsem.at[1])
        own.start()
        own.wait()
        gwo_gather.begin()

    t = s - nblk
    h = t // nblk
    j = t % nblk

    def send_head(h):
        dn_own(h).start()
        for mask in masks:
            dn_copy(h, mask, grid.me).start()
        gw_own(h).start()

    def begin_gw(h):
        gw_own(h).wait()
        dn_own(h).wait()
        gw_gather(h).begin()

    @pl.when((t >= 2 * nblk) & (j == 0))
    def _():
        for mask in masks:
            dn_copy(h - 2, mask, grid.me).wait_send()

    @pl.when((t >= nblk) & (j == 0))
    def _():
        send_head(h - 1)

    @pl.when((t >= nblk) & (j == 1))
    def _():
        begin_gw(h - 1)

    @pl.when((t >= nblk) & (j == FIRST))
    def _():
        gw_gather(h - 1).first()

    @pl.when((t >= nblk) & (j == SECOND))
    def _():
        gw_gather(h - 1).second()

    @pl.when((t >= 2 * nblk) & (j == THIRD))
    def _():
        gw_gather(h - 2).third()

    @pl.when(t == 5)
    def _():
        gwo_gather.first()

    @pl.when(t == 8)
    def _():
        gwo_gather.second()

    @pl.when(t == nblk + THIRD)
    def _():
        gwo_gather.third()

    @pl.when(t >= 0)
    def _():
        rows = pl.ds(pl.multiple_of(h * HD, HD), HD)

        @pl.when(j == 0)
        def _():
            dq_scr[...] = jnp.zeros_like(dq_scr)
            gw_scr[h % 2] = jnp.zeros(gw_scr.shape[1:], F32)

            def augment(data, stat):
                hi, mid, lo = split3(-stat)
                extra = jnp.where(row64 == 0, hi, jnp.where(row64 == 1, mid, jnp.where(row64 == 2, lo, 0.0))).astype(BF16)
                return jnp.concatenate([data, extra], axis=0).T

            def prep(i, carry):
                cols = blk(i)
                do_h = do_scr[rows, cols]
                delta = jnp.sum(do_h.astype(F32) * o_ref[rows, cols].astype(F32), axis=0, keepdims=True)
                qa_scr[cols, :] = augment(q_ref[rows, cols], lse_ref[pl.ds((h // 2) * 8 + h % 2, 1), cols])
                doa_scr[cols, :] = augment(do_h, delta)
                return carry

            lax.fori_loop(0, nblk, prep, 0)

        ones = jnp.where(row64 < 3, 1.0, 0.0).astype(BF16)
        ka_scr[...] = jnp.concatenate([k_ref[rows, :], ones], axis=0)
        va_scr[...] = jnp.concatenate([v_ref[rows, :], ones], axis=0)
        dk_scr[...] = jnp.zeros_like(dk_scr)
        dv_scr[...] = jnp.zeros_like(dv_scr)

        def step(i, masked):
            cols = blk(i)
            scores = dot_nn(qa_scr[cols, :], ka_scr[...])
            if masked:
                qrow = lax.broadcasted_iota(jnp.int32, scores.shape, 0)
                kcol = lax.broadcasted_iota(jnp.int32, scores.shape, 1)
                scores = jnp.where(kcol <= qrow, scores, MASK_VALUE)
            p = jnp.exp2(scores * LOG2E)
            dp = dot_nn(doa_scr[cols, :], va_scr[...])
            ds = (p * dp).astype(BF16)
            dv_scr[...] += dot_nn(do_scr[rows, cols], p.astype(BF16))
            dk_scr[...] += dot_nn(q_ref[rows, cols], ds)
            dq_scr[:, cols] += dot_nt(k_ref[rows, :], ds)

        def body(i, carry):
            step(i, False)
            return carry

        step(j, True)
        lax.fori_loop(j + 1, nblk, body, 0)

        cos = cos_ref[...]
        sin = sin_ref[...]

        def unrope(v, scale):
            v1 = v[0:HD // 2] * scale
            v2 = v[HD // 2:HD] * scale
            return [v1 * cos + v2 * sin, v2 * cos - v1 * sin]

        grads = jnp.concatenate(unrope(dq_scr[:, blk(j)], 0.125) + unrope(dk_scr[...], 1.0) + [dv_scr[...]], axis=0).astype(BF16)
        dn_scr[h % 2, :, blk(j)] = grads
        gw_scr[h % 2] += dot_nn(grads, r_ref[...])

    @pl.when(s == pl.num_programs(0) - 1)
    def _():
        end = HEADS - 1
        send_head(end)
        gw_gather(end - 1).third()
        begin_gw(end)
        gw_gather(end).first()
        gw_gather(end).second()
        gw_gather(end).third()
        for mask in masks:
            o_copy(mask, grid.xor(mask)).wait_recv()
            o_copy(mask, grid.me).wait_send()
            for head in range(HEADS):
                dn_copy(head, mask, grid.xor(mask)).wait_recv()
            for head in range(HEADS - 2, HEADS):
                dn_copy(head, mask, grid.me).wait_send()
        gwo_gather.last()
        for head in range(HEADS):
            gw_gather(head).last()


def bwd_call(dy_all, r_all, q_t, o_t, k_t, v_t, lse, cos_t, sin_t, w_out, o_n):
    seq, hidden = dy_all.shape
    width = q_t.shape[0]
    half = cos_t.shape[0]
    ndev = 8
    piece = seq // ndev
    nblk = seq // BLK
    hbm = pl.BlockSpec(memory_space=pl.ANY)
    whole = lambda *shape: pl.BlockSpec(shape, lambda s: (0, 0), pipeline_mode=pl.Buffered(1))
    jblk = lambda s: lax.rem(s, nblk)
    rblk = lambda s: jnp.where(s < nblk, 0, lax.rem(s, nblk))
    rows = 3 * HD
    dma = pltpu.SemaphoreType.DMA
    return pl.pallas_call(
        bwd_kernel,
        out_shape=(
            jax.ShapeDtypeStruct((ndev, piece, width), BF16),
            jax.ShapeDtypeStruct((ndev * width, hidden), F32),
            jax.ShapeDtypeStruct((HEADS, ndev, rows, piece), BF16),
            jax.ShapeDtypeStruct((ndev, HEADS, rows, hidden), F32),
        ),
        grid=(nblk * (1 + HEADS),),
        in_specs=[
            pl.BlockSpec((BLK, hidden), lambda s: (jnp.minimum(s, nblk - 1), 0)),
            pl.BlockSpec((BLK, hidden), lambda s: (rblk(s), 0)),
            whole(width, seq), whole(width, seq),
            pl.BlockSpec((width, BLK), lambda s: (0, jblk(s))),
            pl.BlockSpec((width, BLK), lambda s: (0, jblk(s))),
            whole(16, seq),
            pl.BlockSpec((half, BLK), lambda s: (0, jblk(s))),
            pl.BlockSpec((half, BLK), lambda s: (0, jblk(s))),
            hbm, hbm,
        ],
        out_specs=(hbm,) * 4,
        scratch_shapes=[
            pltpu.VMEM((width, seq), BF16), pltpu.VMEM((width, hidden), BF16), pltpu.VMEM((width, hidden), F32),
            pltpu.VMEM((seq, 2 * HD), BF16), pltpu.VMEM((seq, 2 * HD), BF16),
            pltpu.VMEM((2 * HD, BLK), BF16), pltpu.VMEM((2 * HD, BLK), BF16),
            pltpu.VMEM((HD, seq), F32), pltpu.VMEM((HD, BLK), F32), pltpu.VMEM((HD, BLK), F32),
            pltpu.VMEM((2, rows, seq), BF16), pltpu.VMEM((2, rows, hidden), F32),
            dma, dma((2,)), dma((8,)), dma((8,)), dma((HEADS, 8)), dma((HEADS, 8)), dma((HEADS + 1, 13)), dma((HEADS + 1, 13)),
        ],
        compiler_params=params(1, collective_id=2, has_side_effects=True),
        cost_estimate=cost(5 * seq * seq * width, seq * hidden * 12, seq * seq),
        name="backward",
    )(dy_all, r_all, q_t, o_t, k_t, v_t, lse, cos_t, sin_t, w_out, o_n)


def place_kernel(gw_ref, out):
    rows = jnp.concatenate([gw_ref[0, h] for h in range(HEADS)], axis=0)
    out[...] = rows.T


def place_call(gw_all):
    ndev, _, rows, hidden = gw_all.shape
    width = HEADS * HD
    return pl.pallas_call(
        place_kernel,
        out_shape=jax.ShapeDtypeStruct((hidden, 3 * ndev * width), F32),
        grid=(3, ndev),
        in_specs=[pl.BlockSpec((1, HEADS, HD, hidden), lambda w, d: (d, 0, w, 0))],
        out_specs=pl.BlockSpec((hidden, width), lambda w, d: (0, w * ndev + d)),
        compiler_params=params(2),
        cost_estimate=cost(1e6, 100e6),
        name="place",
    )(gw_all)


def dx_kernel(dn_ref, wq_ref, wk_ref, wv_ref, x_ref, inv_ref, g_ref, dy_ref, dx_out, gg_out, acc_scr):
    s = pl.program_id(0)
    part = None
    for which, w in enumerate((wq_ref, wk_ref, wv_ref)):
        rhs = jnp.concatenate([dn_ref[h, 0, HD * which:HD * (which + 1)] for h in range(HEADS)], axis=0)
        term = dot_nn(w[...], rhs)
        part = term if part is None else part + term

    @pl.when(s == 0)
    def _():
        acc_scr[...] = part

    @pl.when(s > 0)
    def _():
        acc_scr[...] += part

    @pl.when(s == pl.num_programs(0) - 1)
    def _():
        dn = acc_scr[...].T
        inv = inv_ref[...]
        x_hat = x_ref[...].astype(F32) * inv
        gg_out[...] = jnp.sum(dn * x_hat, axis=0, keepdims=True)
        d_hat = dn * g_ref[...]
        mean = jnp.mean(d_hat * x_hat, axis=-1, keepdims=True)
        dx_out[...] = (dy_ref[...].astype(F32) + inv * (d_hat - x_hat * mean)).astype(BF16)


def dx_call(dn_recv, w_qkv, x, inv_rms, gain, dy):
    _, ndev, rows, piece = dn_recv.shape
    hidden = w_qkv.shape[0]
    width = HEADS * HD
    wspec = lambda which: pl.BlockSpec((hidden, width), lambda s: (0, which * ndev + s))
    whole = lambda *shape: pl.BlockSpec(shape, lambda s: (0, 0), pipeline_mode=pl.Buffered(1))
    return pl.pallas_call(
        dx_kernel,
        out_shape=(jax.ShapeDtypeStruct((piece, hidden), BF16), jax.ShapeDtypeStruct((1, hidden), F32)),
        grid=(ndev,),
        in_specs=[pl.BlockSpec((HEADS, 1, rows, piece), lambda s: (0, s, 0, 0)), wspec(0), wspec(1), wspec(2), whole(piece, hidden), whole(piece, 1), whole(1, hidden), whole(piece, hidden)],
        out_specs=(whole(piece, hidden), whole(1, hidden)),
        scratch_shapes=[pltpu.VMEM((hidden, piece), F32)],
        compiler_params=params(1),
        cost_estimate=cost(2 * piece * hidden * 3 * ndev * width, 40e6),
        name="dx",
    )(dn_recv, w_qkv, w_qkv, w_qkv, x, inv_rms, gain, dy)


def solution(mesh):
    ndev = mesh.shape['cp']

    def device_fn(x_in, positions, long_factor, norm_gain, w_qkv, w_out, grad_y):
        _, piece, hidden = x_in.shape
        seq = piece * ndev
        dev = lax.axis_index('cp').astype(jnp.int32).reshape(1)
        x = x_in[0]
        dy = grad_y[0]
        x_float = x.astype(F32)
        inv_rms = lax.rsqrt(jnp.mean(x_float * x_float, axis=-1, keepdims=True) + NORM_EPS)
        normed = (x_float * inv_rms * norm_gain).astype(BF16)
        half = long_factor.shape[0]
        exponent = jnp.arange(half, dtype=F32) * (1.0 / half)
        inv_freq = 1.0 / (long_factor * jnp.power(10000.0, exponent))
        r_all, q_t, k_t, v_t, k_n, cos_t, sin_t = qkv_call(normed, positions, inv_freq, w_qkv)
        o_t, o_n, lse, dy_all = fwd_call(q_t, k_n, v_t, dy)
        o_recv, g_wout, dn_recv, gw_all = bwd_call(dy_all, r_all, q_t, o_t, k_t, v_t, lse, cos_t, sin_t, w_out, o_n)
        y_out = y_call(dev, o_recv, o_n, w_out, x)
        grad_x, gg = dx_call(dn_recv, w_qkv, x, inv_rms, norm_gain.reshape(1, hidden), dy)
        g_gain = lax.psum(gg.reshape(hidden), 'cp')
        g_wqkv = place_call(gw_all)
        return y_out[None], grad_x[None], g_gain, g_wqkv, g_wout

    seq_spec = P('dp', 'cp', None)
    return jax.shard_map(device_fn, mesh=mesh, in_specs=(seq_spec, P(('dp', 'cp')), P(None), P(None), P(None, None), P(None, None), seq_spec), out_specs=(seq_spec, seq_spec, P('dp'), P('dp', None), P('dp', None)), check_vma=False)
```

time: 5060 us -> 862 us (0.17)
  waiting for transfers between devices: 3990 us -> 0 us
  Pallas kernels: 0 us -> 816 us
  starting transfers between devices: 317 us -> 0 us
  matrix products: 293 us -> 0 us
  local copies, waits for them, and re-layouts: 301 us -> 14.6 us
  other arithmetic: 106 us -> 6.95 us
    ppermute x44 -> x0, waiting for transfers between devices: 3310 us -> none  [the longest x7 2080 us: bwd_step(): k_cur = lax.ppermute(k_cur, 'cp', shift_perm)]
    pallas_call x0 -> x6, Pallas kernels: none -> 816 us  [the longest x1 418 us: bwd_call(): pl.pallas_call(bwd_kernel, out_shape=(jax.ShapeDtypeStruct((ndev, piece,...]
    psum x1 -> x0, waiting for transfers between devices: 680 us -> none  [device_fn(): g_gain, g_wqkv, g_wout = lax.psum((g_gain, g_wqkv, g_wout), 'cp')]
    ppermute x44 -> x0, starting transfers between devices: 317 us -> none  [the longest x7 97 us: fwd_step(): v_cur = lax.ppermute(v_cur, 'cp', shift_perm)]
    dot_general x12 -> x0, matrix products: 293 us -> none  [the longest x1 43.4 us: bwd_block(): jnp.einsum('bqhd,bkhd->bhqk', d_attn, v_blk, preferred_element_type=jnp.f...]
    while x42 -> x0, local copies, waits for them, and re-layouts: 194 us -> none
    unnamed x53 -> x9, local copies, waits for them, and re-layouts: 86.8 us -> 12.4 us
  transfers between devices with their start and end apart: 45 -> 0, of which waited for: 31 -> 0; matrix products, arithmetic and copies ran while one was open for 3% -> 0% of each run, Pallas kernels for 0% -> 0%
where the time goes in v2:
time: 862 us; the launch traced here: 861 us
  Pallas kernels  816 us (95%)
  blocking collectives  22.5 us (3%)
  local copies, waits for them, and re-layouts  14.6 us (2%)
    pallas_call x1, Pallas kernels, bwd_call(): pl.pallas_call(bwd_kernel, out_shape=(jax.ShapeDtypeStruct((ndev, piece,...  418 us
    pallas_call x1, Pallas kernels, fwd_call(): pl.pallas_call(fwd_kernel, out_shape=(jax.ShapeDtypeStruct((width, seq),...  164 us
    pallas_call x1, Pallas kernels, qkv_call(): pl.pallas_call(qkv_kernel, out_shape=(jax.ShapeDtypeStruct((seq, hidden),...  135 us
    pallas_call x1, Pallas kernels, place_call(): pl.pallas_call(place_kernel, out_shape=jax.ShapeDtypeStruct((hidden, 3 *...  45.2 us
    pallas_call x1, Pallas kernels, dx_call(): pl.pallas_call(dx_kernel, out_shape=(jax.ShapeDtypeStruct((piece, hidden)...  36.9 us
    psum x1, blocking collectives, device_fn(): g_gain = lax.psum(gg.reshape(hidden), 'cp')  22.5 us
    pallas_call x1, Pallas kernels, y_call(): pl.pallas_call(y_kernel, out_shape=jax.ShapeDtypeStruct((piece, hidden),...  17.3 us

profile of v2, /device:TPU:0, one launch (start us, length us, event | category | flops | bytes accessed | tf_op | source)
XLA Modules:
  0.0 860.6 jit_solution(6540752646976699510)
XLA Ops:
  0.6 0.0 copy-start.3
  0.6 0.0 copy-start.2
  0.7 2.6 fusion
  3.2 0.0 copy-start
  3.3 0.6 copy-done
  3.8 4.3 fusion.2.r_own
  8.2 0.0 copy-done.3
  8.2 0.7 copy.13.inv_ref
  8.9 0.0 copy-done.2
  8.9 0.6 reshape.46.pos_ref
  9.5 135.0 %gather_qkv.1 = (bf16[6144,2048]{1,0:T(8,128)(2,1)}, bf16[256,6144]{1,0:T(8,128)(2,1)}, bf16[256,6144]{1,0:T(8,128)(2,1)}, bf16[256,6144]{1,0:T(8,128)(2,1)}, bf...) custom-call(bf16[768,2048]{1,0:T(8,128)(2,1)} %fusion.2.r_own, s32[2,1,384]{2,1,0:T(1,128)} %reshape.46.pos_ref, ...), custom_call_target="tpu_custom_call" | custom-call | flops 19327352832 | bytes 62914560 | tf_op jit(solution)/shard_map/gather_qkv/pallas_call | solution.py:270
  144.5 163.6 %attn_fwd.1 = (bf16[256,6144]{1,0:T(8,128)(2,1)}, bf16[6144,256]{1,0:T(8,128)(2,1)}, f32[16,6144]{1,0:T(8,128)}, bf16[6144,2048]{1,0:T(8,128)(2,1)}) custom-call(bf16[256,6144]{1,0:T(8,128)(2,1)} %get-tuple-element.22.q_ref, bf16[6144,256]{1,0:T(8,128)(2,1)} %get-tuple-element.23.k_ref, bf16[256,6144]{1,0:T(8,128)(2,1)} %get-tuple-element.24.v_ref, ...), custom_call_target="tpu_custom_call" | custom-call | flops 77309411328 | bytes 15728640 | tf_op jit(solution)/shard_map/attn_fwd/pallas_call | solution.py:375
  308.1 417.9 %backward.1 = (bf16[8,768,256]{2,1,0:T(8,128)(2,1)}, f32[2048,2048]{1,0:T(8,128)}, bf16[4,8,192,768]{3,2,1,0:T(8,128)(2,1)}, f32[8,4,192,2048]{3,2,1,0:T(8,128)}) custom-call(bf16[6144,2048]{1,0:T(8,128)(2,1)} %get-tuple-element.25.dy_ref, bf16[6144,2048]{1,0:T(8,128)(2,1)} %get-tuple-element.26.r_ref, bf16[256,6144]{1,0:T(8,128)(2,1)} %get-tuple-element.22.q_ref, ...), custom_call_target="tpu_custom_call" | custom-call | flops 48318382080 | bytes 150994944 | tf_op jit(solution)/shard_map/backward/pallas_call | solution.py:664
  726.0 0.0 copy-start.1
  726.0 45.2 %place.1 = f32[2048,6144]{1,0:T(8,128)} custom-call(f32[8,4,192,2048]{3,2,1,0:T(8,128)} %get-tuple-element.37.gw_ref), custom_call_target="tpu_custom_call" | custom-call | flops 1000000 | bytes 100000000 | tf_op jit(solution)/shard_map/place/pallas_call | solution.py:707
  771.2 0.0 copy-done.1
  771.2 0.9 rsqrt.7.inv_ref
  772.2 36.9 %dx.1 = (bf16[768,2048]{1,0:T(8,128)(2,1)}, f32[1,2048]{1,0:T(1,128)}) custom-call(bf16[4,8,192,768]{3,2,1,0:T(8,128)(2,1)} %get-tuple-element.34.dn_ref, bf16[2048,6144]{1,0:T(8,128)(2,1)} %wv_ref.1, bf16[2048,6144]{1,0:T(8,128)(2,1)} %wv_ref.1, bf16[2048,6144]{1,0:T(8,128)(2,1)} %wv_ref.1, bf16[768,2048]{1,0:T(8,128)(2,1)} %bitcast.11, ...), custom_call_target="tpu_custom_call" | custom-call | flops 19327352832 | bytes 40000000 | tf_op jit(solution)/shard_map/dx/pallas_call | solution.py:752
  809.1 22.5 %psum.7 = f32[2048]{0:T(1024)} all-reduce(f32[2048]{0:T(1024)} %bitcast.16), channel_id=1, replica_groups=mesh['dp'=1,'cp'=8] {'cp'}, use_global_device_ids=true, to_apply=%region_1.0 | all-reduce | flops 2048 | bytes 16384 | tf_op jit(solution)/shard_map/psum | solution.py:785
  831.5 17.3 %y_proj.1 = bf16[768,2048]{1,0:T(8,128)(2,1)} custom-call(s32[1]{0:T(128)} %bitcast.d_ref, bf16[8,768,256]{2,1,0:T(8,128)(2,1)} %get-tuple-element.33.o_ref, bf16[6144,256]{1,0:T(8,128)(2,1)} %get-tuple-element.32.on_hbm.own_ref, bf16[2048,2048]{1,0:T(8,128)(2,1)} %w_ref.1, bf16[768,2048]{1,0:T(8,128)(2,1)} %bitcast.12), custom_call_target="tpu_custom_call" | custom-call | flops 6442450944 | bytes 20000000 | tf_op jit(solution)/shard_map/y_proj/pallas_call | solution.py:421
  848.8 11.8 %copy.16 = f32[2048,2048]{1,0:T(8,128)} copy(f32[2048,2048]{1,0:T(8,128)} %get-tuple-element.48) | data formatting | bytes 33554432
  (2 shorter events, 0.0 us)
Async XLA Ops:
  0.6 7.6 copy-start.3
  0.6 8.3 copy-start.2
  3.2 0.6 copy-start
  726.0 45.3 %copy-start.1 = (f32[768]{0:T(1024)S(1)}, f32[768]{0:T(1024)}, u32[]{:S(2)}) copy-start(f32[768]{0:T(1024)} %copy-done) | copy-start | bytes 9220
